TPU v7x, 128 devices: a whole 4x4x4 slice. The times are simulated.
128 devices in a mesh: blk: 128 (over z, x, y, core).
Axes of the slice: x: 4, y: 4, z: 4, core: 2. Of those that a mesh axis runs over, the one named last changes fastest.
Arguments:
- tokens: bfloat16 [65536, 1024], P('blk'), may hold values from -6 to 6
- labels: bfloat16 [65536, 1024], P('blk'), may hold values from -192 to 192
- lengths: int32 [256], P('blk'), may hold values from 1 to 256, as said below
- targets: int32 [65536], P('blk'), may hold values 0 or 1
- w_in: bfloat16 [1024, 2560], replicated, may hold values from -0.1875 to 0.1875
- b_in: float32 [2560], replicated, may hold values from -3 to 3
- w_out: bfloat16 [1024, 1024], replicated, may hold values from -0.1875 to 0.1875
Outputs:
- layer_out: bfloat16 [65536, 1024], P('blk')
- loss: float32 [], replicated
- grad_tokens: bfloat16 [65536, 1024], P('blk')
- grad_in: bfloat16 [1024, 2560], replicated
- grad_bias: float32 [2560], replicated
- grad_out: bfloat16 [1024, 1024], replicated
Inputs may be any that keep to these rules, and one draw needn't show every extreme that they name: `lengths`: some history has exactly 256 used rows.
All inputs are finite; a program needn't handle non-finite values. No bound on the sum of `targets` on one device may be relied on, other than what follows from the above.
Results may differ from a plain program's by a relative error of at most 0.015.
Values may be sent and summed in bfloat16 or wider, within the bound.
No kernel may reach another device: no remote copies, remote signals or barrier semaphores. Data moves between devices by JAX's collectives and lax.ppermute only.
A program may use at most 128 MiB of HBM per device.

v0:
```python
import functools

import jax
import jax.numpy as jnp
from jax import lax
from jax.sharding import Mesh
from jax.sharding import PartitionSpec as P

D = 1024
HEADS = 4
VDIM = 256
QKDIM = 64
LMAX = 256
BLK = ("blk_0", "blk_1", "blk_2", "blk_3")


EPS = 1e-05


def one_axis_at_a_time(x, axes):
    return functools.reduce(lax.psum, axes, x)


def norm_rows(values):
    center = values - jnp.mean(values, axis=-1, keepdims=True)
    spread = jnp.mean(center * center, axis=-1, keepdims=True)
    return center * lax.rsqrt(spread + EPS)


def history_layer(rows, length, w_in, b_in, w_out):
    count_rows = rows.shape[0]
    normed = norm_rows(rows).astype(jnp.bfloat16)
    hidden = jnp.dot(normed, w_in, preferred_element_type=jnp.float32) + b_in
    acts = jax.nn.silu(hidden).astype(jnp.bfloat16)
    width = HEADS * VDIM
    gate = acts[:, :width]
    values = acts[:, width : 2 * width].reshape(count_rows, HEADS, VDIM)
    queries = acts[:, 2 * width : 2 * width + HEADS * QKDIM].reshape(count_rows, HEADS, QKDIM)
    keys = acts[:, 2 * width + HEADS * QKDIM :].reshape(count_rows, HEADS, QKDIM)
    places = lax.iota(jnp.int32, count_rows)
    allowed = (places[None, :] <= places[:, None]) & (places[None, :] < length)
    scores = jnp.einsum("qhe,khe->hqk", queries, keys, preferred_element_type=jnp.float32)
    weights = jnp.where(allowed[None], jax.nn.silu(scores), 0.0).astype(jnp.bfloat16)
    mixed = jnp.einsum("hqk,khe->qhe", weights, values, preferred_element_type=jnp.float32).reshape(
        count_rows, width
    )
    gated = (norm_rows(mixed) * gate.astype(jnp.float32)).astype(jnp.bfloat16)
    full = rows + jnp.dot(gated, w_out, preferred_element_type=jnp.float32)
    return jnp.where((places < length)[:, None], full, 0.0)


def shards(tokens, labels, lengths, targets, w_in, b_in, w_out):
    per_dev = lengths.shape[0]
    home_rows = tokens.reshape(per_dev, LMAX, D)
    places = lax.iota(jnp.int32, LMAX)
    used = places[None, :] < lengths[:, None]
    chosen = (
        (targets.reshape(per_dev, LMAX) == 1) | (places[None, :] == lengths[:, None] - 1)
    ) & used
    local_count = jnp.sum(chosen.astype(jnp.float32))
    home_cot = jnp.where(
        chosen[..., None], labels.reshape(per_dev, LMAX, D), jnp.zeros((), jnp.bfloat16)
    )
    slot_rows, slot_cot, spans = (home_rows, home_cot, lengths)
    block = slot_rows.astype(jnp.float32)
    cot = slot_cot.astype(jnp.float32)

    def forward(rows_in, first_w, bias, second_w):
        return jax.vmap(history_layer, in_axes=(0, 0, None, None, None))(
            rows_in, spans, first_w, bias, second_w
        )

    full, pullback = jax.vjp(forward, block, w_in, b_in, w_out)
    loss_part = jnp.sum(cot * full.astype(jnp.bfloat16).astype(jnp.float32))
    d_rows, d_in, d_bias, d_out = pullback(cot)
    d_in = d_in.astype(jnp.float32)
    d_out = d_out.astype(jnp.float32)
    home_full, home_grad = (full, d_rows)
    bias_sum, loss_sum, total = (
        one_axis_at_a_time(d_bias, BLK),
        one_axis_at_a_time(loss_part, BLK),
        one_axis_at_a_time(local_count, BLK),
    )
    grad_tokens = (home_grad / total).astype(jnp.bfloat16).reshape(per_dev * LMAX, D)
    sum_in, sum_out = lax.psum((d_in, d_out), BLK)
    grad_in = (sum_in / total).astype(jnp.bfloat16)
    grad_out = (sum_out / total).astype(jnp.bfloat16)
    layer_out = home_full.astype(jnp.bfloat16).reshape(per_dev * LMAX, D)
    return (layer_out, loss_sum / total, grad_tokens, grad_in, bias_sum / total, grad_out)


def solution(mesh):
    torus = Mesh(mesh.devices.reshape(4, 4, 4, 2), ("blk_0", "blk_1", "blk_2", "blk_3"))
    placed = (P(BLK, None), P(BLK, None), P(BLK), P(BLK), P(), P(), P())
    return jax.shard_map(
        shards,
        mesh=torus,
        in_specs=placed,
        out_specs=(P(BLK, None), P(), P(BLK, None), P(), P(), P()),
        check_vma=False,
    )
```

profile of v0, /device:TPU:1, one launch (start us, length us, event | category | flops | bytes accessed | tf_op | source)
XLA Modules:
  0.0 271.1 jit_solution(17990621672282603548)
XLA Ops:
  7.2 0.0 all-reduce.11.cloned.1.call-start
  7.3 0.8 broadcast_add_fusion.1
  8.1 0.8 iota_compare_fusion.2
  8.8 1.4 convert_reduce_fusion
  10.3 1.6 multiply_reduce_fusion.1
  12.0 7.4 %multiply_convert_fusion = (bf16[2,256,2560]{2,1,0:T(8,128)(2,1)S(1)}, f32[2,256,2560]{2,1,0:T(8,128)}) fusion(f32[2560]{0:T(1024)S(1)} %copy-done.17, bf16[1024,2560]{1,0:T(8,128)(2,1)} %param.11, f32[2,256]{1,0:T(2,128)S(1)} %rsqrt.20, f32[2,256]{1,0:T(2,128)S(1)} %div.74, bf16[2,256,1024]{2,1,0:T(8,128)(2,1)S(1)} %bitcast.82), kind=kOutput, calls=%fused_computation.12 | convolution fusion | flops 2694316032 | bytes 14170112 | tf_op jit(solution)/shard_map/jvp(vmap())/dot_general | solution.py:33
  19.5 0.8 fusion.53
  20.3 0.8 copy-done.4
  21.1 1.1 slice.16
  22.3 0.1 iota_compare_fusion.1
  22.4 0.6 convert_reduce_fusion.1
  23.0 0.6 or_and_fusion
  23.6 0.1 broadcast_and_fusion
  23.7 1.1 copy.28
  24.8 1.8 copy.27
  26.6 1.5 fusion.56
  28.1 0.9 bitcast_reduce_fusion
  29.0 0.4 copy-done.11
  29.4 1.3 copy-done.3
  30.7 0.8 fusion.23
  31.6 2.9 %copy.42 = f32[2,256,1024]{2,1,0:T(8,128)} copy(f32[2,256,1024]{1,2,0:T(8,128)} %bitcast.87) | data formatting | bytes 4194304 | tf_op jit(solution)/shard_map/jvp(vmap())/reshape | solution.py:44
  34.5 3.8 %multiply_reduce_fusion = (f32[2,256]{1,0:T(2,128)S(1)}, bf16[2,256,1024]{2,1,0:T(8,128)(2,1)S(1)}) fusion(f32[2,256,1024]{2,1,0:T(8,128)} %copy.42, f32[2,256]{1,0:T(2,128)S(1)} %broadcast_multiply_fusion, bf16[2,256,2560]{2,1,0:T(8,128)(2,1)} %copy-done.4, bf16[1024,1024]{1,0:T(8,128)(2,1)S(1)} %copy-done, pred[2,256]{1,0:T(4,128)(4,1)} %copy-done.20, ...), kind=kOutput, calls=%fused_computation.45 | convolution fusion | flops 1078984192 | bytes 7345152 | tf_op jit(solution)/shard_map/transpose(jvp(vmap()))/dot_general | solution.py:48
  38.4 2.4 fusion.45
  40.8 1.7 broadcast_add_fusion
  42.5 2.3 copy.43
  44.8 3.5 %fusion.17 = bf16[2,4,256,256]{3,2,1,0:T(8,128)(2,1)S(1)} fusion(f32[2,4,256,256]{3,2,1,0:T(8,128)} %copy-done.11, bf16[2,4,256,256]{3,2,1,0:T(8,128)(2,1)} %bitcast.95, pred[2,256,256]{2,1,0:T(8,128)(4,1)S(1)} %broadcast_and_fusion, bf16[2,32,4,8,256]{4,3,2,1,0:T(8,128)(2,1)} %bitcast.92), kind=kOutput, calls=%fused_computation.36 | convolution fusion | flops 274726912 | bytes 5373952 | tf_op jit(solution)/shard_map/transpose(jvp(vmap(hqk,khe->qhe)))/dot_general | solution.py:44
  48.4 1.8 convolution_convert_fusion
  50.2 1.2 fusion.57
  51.3 1.0 fusion.58
  52.3 2.3 copy.44
  54.6 1.1 copy.34
  55.7 1.8 copy.35
  57.5 5.1 %fusion.18 = f32[1024,1024]{1,0:T(8,128)} fusion(bf16[2,256,1024]{2,1,0:T(8,128)(2,1)} %get-tuple-element.25, pred[2,256]{1,0:T(4,128)(4,1)S(1)} %copy-done.21, bf16[2,256,1024]{2,1,0:T(8,128)(2,1)} %bitcast.100, pred[2,256]{1,0:T(4,128)(4,1)S(1)} %copy-done.22), kind=kOutput, calls=%fused_computation.37 | convolution fusion | flops 1077411840 | bytes 6292480 | tf_op jit(solution)/shard_map/transpose(jvp(vmap()))/dot_general | solution.py:48
  62.6 4.4 %fusion.51 = (f32[2560]{0:T(1024)S(1)}, bf16[2,256,2560]{2,1,0:T(8,128)(2,1)S(1)}) fusion(f32[2,256,2560]{2,1,0:T(8,128)} %get-tuple-element.32, f32[2560]{0:T(1024)S(1)} %copy-done.18, bf16[2,256,1024]{2,1,0:T(8,128)(2,1)S(1)} %copy-done.8, bf16[2,256,1024]{2,1,0:T(8,128)(2,1)S(1)} %copy-done.6, bf16[2,256,256]{2,1,0:T(8,128)(2,1)S(1)} %copy-done.13, ...), kind=kLoop, calls=%fused_computation.96 | loop fusion | flops 26211840 | bytes 10506240 | tf_op jit(solution)/shard_map/transpose(jvp(vmap()))/reduce_sum | solution.py:33
  67.0 1.5 copy-done.9
  68.5 5.6 %fusion = f32[1024,2560]{1,0:T(8,128)} fusion(bf16[2,256,2560]{2,1,0:T(8,128)(2,1)S(1)} %get-tuple-element.21, f32[2,256]{1,0:T(2,128)S(1)} %rsqrt.20, f32[2,256]{1,0:T(2,128)S(1)} %div.74, bf16[2,256,1024]{2,1,0:T(8,128)(2,1)S(1)} %bitcast.83), kind=kOutput, calls=%fused_computation.5 | convolution fusion | flops 2689073152 | bytes 14159872 | tf_op jit(solution)/shard_map/transpose(jvp(vmap()))/dot_general | solution.py:33
  74.1 4.5 %fusion.13 = (f32[]{:T(128)}, bf16[2,256,1024]{2,1,0:T(8,128)(2,1)}) fusion(bf16[2,256,1024]{2,1,0:T(8,128)(2,1)} %bitcast.101, pred[2,256]{1,0:T(4,128)(4,1)S(1)} %copy-done.22, bf16[2,256,1024]{2,1,0:T(8,128)(2,1)} %get-tuple-element.25, bf16[1024,1024]{1,0:T(8,128)(2,1)S(1)} %copy-done, pred[2,256]{1,0:T(4,128)(4,1)S(1)} %copy-done.21, ...), kind=kOutput, calls=%fused_computation.32 | convolution fusion | flops 1078460416 | bytes 6292484 | tf_op jit(solution)/shard_map/jvp(vmap())/dot_general | solution.py:48
  78.6 17.6 %all-reduce.7 = (f32[]{:T(128)}, f32[]{:T(128)}, f32[2560]{0:T(1024)S(1)}) all-reduce(f32[]{:T(128)} %get-tuple-element.37, f32[]{:T(128)} %get-tuple-element.22, f32[2560]{0:T(1024)S(1)} %get-tuple-element.20), channel_id=1, replica_groups=mesh['blk_0'=4,'blk_1'=4,'blk_2'=4,'blk_3'=2] {'blk_0'}, use_global_device_ids=true, to_apply=%region_5.6 | all-reduce | flops 2562 | bytes 20496 | tf_op jit(solution)/shard_map/psum | solution.py:21
  96.2 15.8 %all-reduce.6 = (f32[]{:T(128)}, f32[]{:T(128)}, f32[2560]{0:T(1024)S(1)}) all-reduce(f32[]{:T(128)} %get-tuple-element.14, f32[]{:T(128)} %get-tuple-element.15, f32[2560]{0:T(1024)S(1)} %get-tuple-element.16), channel_id=1, replica_groups=mesh['blk_0'=4,'blk_1'=4,'blk_2'=4,'blk_3'=2] {'blk_1'}, use_global_device_ids=true, to_apply=%region_6.7 | all-reduce | flops 2562 | bytes 20496 | tf_op jit(solution)/shard_map/psum | solution.py:21
  112.0 14.8 %all-reduce.5 = (f32[]{:T(128)}, f32[]{:T(128)}, f32[2560]{0:T(1024)S(1)}) all-reduce(f32[]{:T(128)} %get-tuple-element.11, f32[]{:T(128)} %get-tuple-element.12, f32[2560]{0:T(1024)S(1)} %get-tuple-element.13), channel_id=1, replica_groups=mesh['blk_0'=4,'blk_1'=4,'blk_2'=4,'blk_3'=2] {'blk_2'}, use_global_device_ids=true, to_apply=%region_7.8 | all-reduce | flops 2562 | bytes 20496 | tf_op jit(solution)/shard_map/psum | solution.py:21
  126.7 13.5 %all-reduce.8 = (f32[]{:T(128)}, f32[]{:T(128)}, f32[2560]{0:T(1024)S(1)}) all-reduce(f32[]{:T(128)} %get-tuple-element.8, f32[]{:T(128)} %get-tuple-element.9, f32[2560]{0:T(1024)S(1)} %get-tuple-element.10), channel_id=1, replica_groups=mesh['blk_0'=4,'blk_1'=4,'blk_2'=4,'blk_3'=2] {'blk_3'}, use_global_device_ids=true, to_apply=%region_8.9 | all-reduce | flops 2562 | bytes 20496 | tf_op jit(solution)/shard_map/psum | solution.py:21
  141.6 6.4 %fusion.15 = (f32[2,256]{1,0:T(2,128)S(1)}, bf16[2,256,1024]{2,1,0:T(8,128)(2,1)S(1)}) fusion(f32[2,256]{1,0:T(2,128)S(1)} %div.74, bf16[2,256,2560]{2,1,0:T(8,128)(2,1)} %copy-done.9, bf16[1024,2560]{1,0:T(8,128)(2,1)} %param.11, bf16[2,256,1024]{2,1,0:T(8,128)(2,1)S(1)} %bitcast.85), kind=kOutput, calls=%fused_computation.34 | convolution fusion | flops 2686975488 | bytes 9965568 | tf_op jit(solution)/shard_map/transpose(jvp(vmap()))/dot_general | solution.py:33
  148.0 0.7 fusion.40
  148.8 1.3 broadcast_divide_fusion
  150.0 2.8 %fusion.24 = bf16[2,256,1024]{2,1,0:T(8,128)(2,1)} fusion(f32[]{:T(128)} %get-tuple-element.18, f32[2,256]{1,0:T(2,128)S(1)} %negate_multiply_fusion, pred[2,256]{1,0:T(4,128)(4,1)S(1)} %copy-done.21, f32[2,256]{1,0:T(2,128)S(1)} %multiply_multiply_fusion, f32[2,256]{1,0:T(2,128)S(1)} %div.74, f32[2,256]{1,0:T(2,128)S(1)} %rsqrt.20, ...), kind=kLoop, calls=%fused_computation.51 | loop fusion | flops 7340032 | bytes 4203524 | tf_op jit(solution)/shard_map/convert_element_type | solution.py:84
  152.8 99.1 %all-reduce.11.cloned.1.call-done = (f32[1024,2560]{1,0:T(8,128)}, f32[1024,1024]{1,0:T(8,128)}) async-done(((f32[1024,2560]{1,0:T(8,128)}, f32[1024,1024]{1,0:T(8,128)}), (f32[1024,2560]{1,0:T(8,128)}, f32[1024,1024]{1,0:T(8,128)})) %all-reduce.11.cloned.1.call-update) | async-done | bytes 14680080 | tf_op jit(solution)/shard_map/psum | solution.py:85
  251.9 8.6 %divide_convert_fusion = bf16[1024,2560]{1,0:T(8,128)(2,1)} fusion(f32[1024,2560]{1,0:T(8,128)} %get-tuple-element.6, f32[]{:T(128)} %get-tuple-element.18), kind=kLoop, calls=%fused_computation.1 | loop fusion | flops 5242880 | bytes 15728644 | tf_op jit(solution)/shard_map/convert_element_type | solution.py:86
  260.6 2.6 divide_convert_fusion.1
  (61 shorter events, 0.3 us)
Async XLA Ops:
  7.2 27.3 %copy-start = (bf16[1024,1024]{1,0:T(8,128)(2,1)S(1)}, bf16[1024,1024]{1,0:T(8,128)(2,1)}, u32[]{:S(2)}) copy-start(bf16[1024,1024]{1,0:T(8,128)(2,1)} %param.13) | copy-start | bytes 6291460
  7.2 4.8 %copy-start.2 = (bf16[512,1024]{1,0:T(8,128)(2,1)S(1)}, bf16[512,1024]{1,0:T(8,128)(2,1)}, u32[]{:S(2)}) copy-start(bf16[512,1024]{1,0:T(8,128)(2,1)} %param.7) | copy-start | bytes 3145732
  7.2 4.8 %copy-start.17 = (f32[2560]{0:T(1024)S(1)}, f32[2560]{0:T(1024)}, u32[]{:S(2)}) copy-start(f32[2560]{0:T(1024)} %param.12) | copy-start | bytes 30724
  7.2 244.7 %all-reduce.11.cloned.1.call-start = ((), (), s32[]{:S(2)}) async-start(), calls=%async_computation | async-start | bytes 29360128 | tf_op jit(solution)/shard_map/psum | solution.py:85
  8.8 14.8 %copy-start.20 = (pred[2,256]{1,0:T(4,128)(4,1)}, pred[2,256]{1,0:T(4,128)(4,1)S(1)}, u32[]{:S(2)}) copy-start(pred[2,256]{1,0:T(4,128)(4,1)S(1)} %iota_compare_fusion.2) | copy-start | bytes 1540
  19.5 1.7 copy-start.4
  19.5 2.9 %copy-start.23 = (s32[512]{0:T(512)S(1)}, s32[512]{0:T(512)}, u32[]{:S(2)}) copy-start(s32[512]{0:T(512)} %param.10) | copy-start | bytes 6148
  19.5 3.5 %copy-start.24 = (s32[2]{0:T(128)S(1)}, s32[2]{0:T(128)}, u32[]{:S(2)}) copy-start(s32[2]{0:T(128)} %param.9) | copy-start | bytes 28
  26.6 1.5 copy-start.14
  28.1 1.3 copy-start.11
  29.4 1.3 copy-start.3
  34.5 3.9 %copy-start.19 = (f32[2,256]{1,0:T(2,128)S(1)}, f32[2,256]{1,0:T(2,128)}, u32[]{:S(2)}) copy-start(f32[2,256]{1,0:T(2,128)} %fusion.23) | copy-start | bytes 6148
  34.5 3.9 %copy-start.1 = (f32[2,256,1024]{2,1,0:T(8,128)S(1)}, f32[2,256,1024]{2,1,0:T(8,128)}, u32[]{:S(2)}) copy-start(f32[2,256,1024]{2,1,0:T(8,128)} %copy.42) | copy-start | bytes 6291460
  34.5 3.9 %copy-start.5 = (bf16[2,256,2560]{2,1,0:T(8,128)(2,1)S(1)}, bf16[2,256,2560]{2,1,0:T(8,128)(2,1)}, u32[]{:S(2)}) copy-start(bf16[2,256,2560]{2,1,0:T(8,128)(2,1)} %copy-done.4) | copy-start | bytes 7864324
  44.8 3.5 %copy-start.12 = (f32[2,4,256,256]{3,2,1,0:T(8,128)S(1)}, f32[2,4,256,256]{3,2,1,0:T(8,128)}, u32[]{:S(2)}) copy-start(f32[2,4,256,256]{3,2,1,0:T(8,128)} %copy-done.11) | copy-start | bytes 6291460
  44.8 3.5 %copy-start.15 = (bf16[2,256,1024]{1,2,0:T(8,128)(2,1)S(1)}, bf16[2,256,1024]{1,2,0:T(8,128)(2,1)}, u32[]{:S(2)}) copy-start(bf16[2,256,1024]{1,2,0:T(8,128)(2,1)} %copy.43) | copy-start | bytes 3145732
  48.3 3.0 %copy-start.10 = (bf16[2,256,256]{1,2,0:T(8,128)(2,1)S(1)}, bf16[2,256,256]{1,2,0:T(8,128)(2,1)}, u32[]{:S(2)}) copy-start(bf16[2,256,256]{1,2,0:T(8,128)(2,1)} %copy.27) | copy-start | bytes 786436
  51.3 6.2 %copy-start.21 = (pred[2,256]{1,0:T(4,128)(4,1)S(1)}, pred[2,256]{1,0:T(4,128)(4,1)}, u32[]{:S(2)}) copy-start(pred[2,256]{1,0:T(4,128)(4,1)} %copy-done.20) | copy-start | bytes 1540
  51.3 6.2 %copy-start.22 = (pred[2,256]{1,0:T(4,128)(4,1)S(1)}, pred[2,256]{1,0:T(4,128)(4,1)}, u32[]{:S(2)}) copy-start(pred[2,256]{1,0:T(4,128)(4,1)} %or_and_fusion) | copy-start | bytes 1540
  57.5 5.1 %copy-start.6 = (bf16[2,256,1024]{2,1,0:T(8,128)(2,1)S(1)}, bf16[2,256,1024]{2,1,0:T(8,128)(2,1)}, u32[]{:S(2)}) copy-start(bf16[2,256,1024]{2,1,0:T(8,128)(2,1)} %copy.44) | copy-start | bytes 3145732
  57.5 5.1 %copy-start.8 = (bf16[2,256,1024]{2,1,0:T(8,128)(2,1)S(1)}, bf16[2,256,1024]{2,1,0:T(8,128)(2,1)}, u32[]{:S(2)}) copy-start(bf16[2,256,1024]{2,1,0:T(8,128)(2,1)} %get-tuple-element.26) | copy-start | bytes 3145732
  57.5 5.1 %copy-start.13 = (bf16[2,256,256]{2,1,0:T(8,128)(2,1)S(1)}, bf16[2,256,256]{2,1,0:T(8,128)(2,1)}, u32[]{:S(2)}) copy-start(bf16[2,256,256]{2,1,0:T(8,128)(2,1)} %copy.35) | copy-start | bytes 786436
  57.5 5.1 %copy-start.18 = (f32[2560]{0:T(1024)S(1)}, f32[2560]{0:T(1024)}, u32[]{:S(2)}) copy-start(f32[2560]{0:T(1024)} %param.12) | copy-start | bytes 30724
  67.0 1.5 copy-start.9
  148.0 2.0 copy-start.16
  251.9 8.6 %copy-start.7 = (f32[1024,1024]{1,0:T(8,128)S(1)}, f32[1024,1024]{1,0:T(8,128)}, u32[]{:S(2)}) copy-start(f32[1024,1024]{1,0:T(8,128)} %get-tuple-element.7) | copy-start | bytes 12582916
Sparse Core Ops, SparseCore 0:
  74.2 177.6 all-reduce.10
where the time goes:
time: 272 us; the launch traced here: 271 us
  waiting for transfers between devices  99.2 us (36%)
  blocking collectives  61.6 us (23%)
  matrix products  42.8 us (16%)
  other arithmetic  31.3 us (12%)
  local copies, waits for them, and re-layouts  19.4 us (7%)
  between operations  16.8 us (6%)
    psum x1, waiting for transfers between devices, shards(): sum_in, sum_out = lax.psum((d_in, d_out), BLK)  99.1 us
    psum x4, blocking collectives, one_axis_at_a_time(): return functools.reduce(lax.psum, axes, x)  61.6 us
    dot_general x3, matrix products, history_layer(): hidden = jnp.dot(normed, w_in, preferred_element_type=jnp.float32) + b_in  19.4 us
    dot_general x3, matrix products, history_layer(): full = rows + jnp.dot(gated, w_out, preferred_element_type=jnp.float32)  13.4 us
    convert_element_type x1, other arithmetic, shards(): grad_in = (sum_in / total).astype(jnp.bfloat16)  8.62 us
    dot_general x3, matrix products, history_layer(): jnp.einsum('hqk,khe->qhe', weights, values, preferred_element_type=jnp.fl...  6.21 us
  transfers between devices with their start and end apart: 1, of which 1 were waited for; matrix products, arithmetic and copies ran while one was open for 6% of the time, Pallas kernels for 0%

commit v1 on v0

v1 whole, which is shorter than its diff:
```python
import functools

import jax
import jax.numpy as jnp
from jax import lax
from jax.experimental import pallas as pl
from jax.experimental.pallas import tpu as pltpu
from jax.sharding import Mesh
from jax.sharding import PartitionSpec as P

D = 1024
HEADS = 4
VDIM = 256
QKDIM = 64
LMAX = 256
COLS = 2560
ROWS = 512
QCOL = 2048
KCOL = 2304
AXES = ("z", "x", "y", "c")
CHIPS = ("z", "x", "y")
PIECES = 64
BLOCKS = 14
DATA = BLOCKS * 16
PIECE = DATA + 8
EPS = 1e-05
F32 = jnp.float32
BF16 = jnp.bfloat16
INTERPRET = False


def sigmoid(h):
    return 0.5 * jnp.tanh(0.5 * h) + 0.5


def nn(a, b):
    return jnp.dot(a, b, preferred_element_type=F32)


def nt(a, b):
    return lax.dot_general(a, b, (((1,), (1,)), ((), ())), preferred_element_type=F32)


def tn(a, b):
    return lax.dot_general(a, b, (((0,), (0,)), ((), ())), preferred_element_type=F32)


def three_parts(value):
    hi = value.astype(BF16).astype(F32)
    rest = value - hi
    mid = rest.astype(BF16).astype(F32)
    low = (rest - mid).astype(BF16).astype(F32)
    return hi, mid, low


def row_stats(x):
    center = x - jnp.mean(x, axis=-1, keepdims=True)
    spread = jnp.mean(center * center, axis=-1, keepdims=True)
    return center, lax.rsqrt(spread + EPS)


def allowed_mask(length):
    i = lax.broadcasted_iota(jnp.int32, (LMAX, LMAX), 0)
    j = lax.broadcasted_iota(jnp.int32, (LMAX, LMAX), 1)
    return (j <= i) & (j < length)


def local_kernel(
    meta, tgt, tok, lab, win, bias, wout,
    out, dx, mine, send,
    hid, normed, normed_t, acts, dh, mixed, gated_t, dm, sc, wt, cot, inv_s, dqk, bsum, lsum, csum, ext, pay, sems,
):
    core = meta[2]
    bsum[...] = jnp.zeros_like(bsum)
    lsum[...] = jnp.zeros_like(lsum)
    csum[...] = jnp.zeros_like(csum)

    def prologue(r, carry):
        rows = pl.ds(pl.multiple_of(r * 128, 128), 128)
        length = meta[r // 2]
        place = (r % 2) * 128 + lax.broadcasted_iota(jnp.int32, (128, 128), 0)
        marks = jnp.transpose(jnp.broadcast_to(tgt[pl.ds(r, 1), :].astype(F32), (128, 128)))
        chosen = ((marks == 1.0) | (place == length - 1)) & (place < length)
        flag = jnp.where(chosen, 1.0, 0.0)
        csum[...] += jnp.sum(flag, axis=0, keepdims=True)
        wide = jnp.concatenate([flag] * 8, axis=1)
        cot[rows, :] = jnp.where(wide > 0.0, lab[rows, :].astype(F32), 0.0).astype(BF16)
        center, inv = row_stats(tok[rows, :].astype(F32))
        y = center * inv
        normed[rows, :] = y.astype(BF16)
        normed_t[:, rows] = jnp.transpose(y).astype(BF16)
        return carry

    lax.fori_loop(0, 4, prologue, 0)

    def project(c, carry):
        cols = pl.ds(pl.multiple_of(c * 512, 512), 512)
        h = nn(normed[...], win[:, cols]) + bias[:, cols]
        hid[:, cols] = h
        acts[:, cols] = (h * sigmoid(h)).astype(BF16)
        return carry

    lax.fori_loop(0, 5, project, 0)

    for n in range(2):
        rows = slice(n * LMAX, (n + 1) * LMAX)
        allowed = allowed_mask(meta[n])
        for h in range(HEADS):
            q = acts[rows, QCOL + h * QKDIM : QCOL + (h + 1) * QKDIM]
            k = acts[rows, KCOL + h * QKDIM : KCOL + (h + 1) * QKDIM]
            v = acts[rows, D + h * VDIM : D + (h + 1) * VDIM]
            s = nt(q, k)
            w = jnp.where(allowed, s * sigmoid(s), 0.0).astype(BF16)
            sc[n * HEADS + h] = s
            wt[n * HEADS + h] = w
            mixed[rows, h * VDIM : (h + 1) * VDIM] = nn(w, v)

    def gate(r, carry):
        rows = pl.ds(pl.multiple_of(r * 128, 128), 128)
        center, inv = row_stats(mixed[rows, :])
        y = center * inv
        mixed[rows, :] = y
        inv_s[rows, :] = jnp.broadcast_to(inv, (128, 128))
        gated = (y * acts[rows, :D].astype(F32)).astype(BF16)
        gated_t[:, rows] = jnp.transpose(gated.astype(F32)).astype(BF16)
        length = meta[r // 2]
        place = (r % 2) * 128 + lax.broadcasted_iota(jnp.int32, (128, D), 0)
        full = tok[rows, :].astype(F32) + nn(gated, wout[...])
        rounded = jnp.where(place < length, full, 0.0).astype(BF16)
        out[rows, :] = rounded
        c = cot[rows, :]
        lsum[...] += jnp.sum(c.astype(F32) * rounded.astype(F32), axis=0, keepdims=True)
        dg = nt(c, wout[...]).astype(BF16).astype(F32)
        u = acts[rows, :D].astype(F32)
        dy = dg * u
        du = (dg * y).astype(BF16).astype(F32)
        m1 = jnp.mean(dy, axis=-1, keepdims=True)
        m2 = jnp.mean(dy * y, axis=-1, keepdims=True)
        dm[rows, :] = (inv * (dy - m1 - y * m2)).astype(BF16)
        hu = hid[rows, :D]
        sg = sigmoid(hu)
        dhu = du * (sg * (1.0 + hu * (1.0 - sg)))
        dh[rows, :D] = dhu.astype(BF16)
        bsum[0:1, :D] += jnp.sum(dhu, axis=0, keepdims=True)
        return carry

    lax.fori_loop(0, 4, gate, 0)

    def store(j, value):
        half, jj = j // BLOCKS, j % BLOCKS
        pay[half, :, jj * 16 : (jj + 1) * 16, :] = value.astype(BF16).reshape(PIECES, 16, 128)

    for c in range(2):
        g = nn(gated_t[...], cot[:, c * 512 : (c + 1) * 512])
        for i in range(4):
            store(20 + 4 * c + i, g[:, i * 128 : (i + 1) * 128])

    for n in range(2):
        rows = slice(n * LMAX, (n + 1) * LMAX)
        allowed = allowed_mask(meta[n])
        for h in range(HEADS):
            q = acts[rows, QCOL + h * QKDIM : QCOL + (h + 1) * QKDIM]
            k = acts[rows, KCOL + h * QKDIM : KCOL + (h + 1) * QKDIM]
            vc = slice(D + h * VDIM, D + (h + 1) * VDIM)
            d = dm[rows, h * VDIM : (h + 1) * VDIM]
            dw = nt(d, acts[rows, vc]).astype(BF16).astype(F32)
            dv = tn(wt[n * HEADS + h], d).astype(BF16).astype(F32)
            s = sc[n * HEADS + h]
            sg = sigmoid(s)
            ds = jnp.where(allowed, dw * (sg * (1.0 + s * (1.0 - sg))), 0.0).astype(BF16)
            dqk[rows, h * QKDIM : (h + 1) * QKDIM] = nn(ds, k)
            dqk[rows, 256 + h * QKDIM : 256 + (h + 1) * QKDIM] = tn(ds, q)
            hv = hid[rows, vc]
            sg = sigmoid(hv)
            dhv = dv * (sg * (1.0 + hv * (1.0 - sg)))
            dh[rows, vc] = dhv.astype(BF16)
            bsum[0:1, vc] += jnp.sum(dhv, axis=0, keepdims=True)
        hq = hid[rows, QCOL:]
        sg = sigmoid(hq)
        dhq = dqk[rows, :].astype(BF16).astype(F32) * (sg * (1.0 + hq * (1.0 - sg)))
        dh[rows, QCOL:] = dhq.astype(BF16)
        bsum[0:1, QCOL:] += jnp.sum(dhq, axis=0, keepdims=True)

    for c in range(5):
        g = nn(normed_t[...], dh[:, c * 512 : (c + 1) * 512])
        for i in range(4):
            store(4 * c + i, g[:, i * 128 : (i + 1) * 128])

    ext[...] = jnp.zeros_like(ext)
    for j in range(COLS // 128):
        parts = three_parts(bsum[0:1, j * 128 : (j + 1) * 128])
        base = 8 * (j // 2) + j % 2
        for t in range(3):
            ext[base + 2 * t : base + 2 * t + 1, :] = parts[t]
    loss = jnp.sum(lsum[...], axis=1, keepdims=True)
    lane = lax.broadcasted_iota(jnp.int32, (1, 128), 1)
    tail = jnp.where(lane == 0, jnp.broadcast_to(loss, (1, 128)), jnp.where(lane == 1, csum[...], 0.0))
    parts = three_parts(tail)
    for t in range(3):
        ext[80 + 2 * t : 81 + 2 * t, :] = parts[t]
    for half in range(2):
        pay[half, :, DATA:, :] = jnp.zeros((PIECES, 8, 128), BF16)
        for p in range(11):
            pay[half, p, DATA:, :] = ext[8 * p : 8 * p + 8, :].astype(BF16)

    to_send = pltpu.make_async_copy(pay.at[1 - core], send, sems.at[0])
    to_keep = pltpu.make_async_copy(pay.at[core], mine, sems.at[1])
    to_send.start()
    to_keep.start()

    def back(r, carry):
        rows = pl.ds(pl.multiple_of(r * 128, 128), 128)
        dn = nt(dh[rows, :], win[...]).astype(BF16).astype(F32)
        center, inv = row_stats(tok[rows, :].astype(F32))
        y = center * inv
        m1 = jnp.mean(dn, axis=-1, keepdims=True)
        m2 = jnp.mean(dn * y, axis=-1, keepdims=True)
        dx[rows, :] = inv * (dn - m1 - y * m2) + cot[rows, :].astype(F32)
        return carry

    lax.fori_loop(0, 4, back, 0)
    to_send.wait()
    to_keep.wait()


def local_step(meta, tgt, tok, lab, win, bias, wout):
    vm = pl.BlockSpec(memory_space=pltpu.VMEM)
    hbm = pl.BlockSpec(memory_space=pl.ANY)
    half = jax.ShapeDtypeStruct((PIECES, PIECE, 128), BF16)
    return pl.pallas_call(
        local_kernel,
        in_specs=[pl.BlockSpec(memory_space=pltpu.SMEM)] + [vm] * 6,
        out_specs=[vm, vm, hbm, hbm],
        out_shape=[
            jax.ShapeDtypeStruct((ROWS, D), BF16),
            jax.ShapeDtypeStruct((ROWS, D), F32),
            half,
            half,
        ],
        scratch_shapes=[
            pltpu.VMEM((ROWS, COLS), F32),
            pltpu.VMEM((ROWS, D), BF16),
            pltpu.VMEM((D, ROWS), BF16),
            pltpu.VMEM((ROWS, COLS), BF16),
            pltpu.VMEM((ROWS, COLS), BF16),
            pltpu.VMEM((ROWS, D), F32),
            pltpu.VMEM((D, ROWS), BF16),
            pltpu.VMEM((ROWS, D), BF16),
            pltpu.VMEM((2 * HEADS, LMAX, LMAX), F32),
            pltpu.VMEM((2 * HEADS, LMAX, LMAX), BF16),
            pltpu.VMEM((ROWS, D), BF16),
            pltpu.VMEM((ROWS, 128), F32),
            pltpu.VMEM((ROWS, 512), F32),
            pltpu.VMEM((8, COLS), F32),
            pltpu.VMEM((1, D), F32),
            pltpu.VMEM((1, 128), F32),
            pltpu.VMEM((88, 128), F32),
            pltpu.VMEM((2, PIECES, PIECE, 128), BF16),
            pltpu.SemaphoreType.DMA((2,)),
        ],
        compiler_params=pltpu.CompilerParams(vmem_limit_bytes=58 * 2**20),
        interpret=INTERPRET,
        name="local_step",
    )(meta, tgt, tok, lab, win, bias, wout)


def resplit(total):
    value = total[..., 0:2, :] + total[..., 2:4, :] + total[..., 4:6, :]
    hi, mid, low = three_parts(value)
    return jnp.concatenate([hi, mid, low, jnp.zeros_like(hi)], axis=-2)


def pair_kernel(a, b, o):
    o[:, :DATA, :] = (a[:, :DATA, :].astype(F32) + b[:, :DATA, :].astype(F32)).astype(BF16)
    o[:, DATA:, :] = resplit(a[:, DATA:, :].astype(F32) + b[:, DATA:, :].astype(F32)).astype(BF16)


def pair_add(a, b):
    spec = pl.BlockSpec((8, PIECE, 128), lambda i: (i, 0, 0))
    return pl.pallas_call(
        pair_kernel,
        grid=(PIECES // 8,),
        in_specs=[spec, spec],
        out_specs=spec,
        out_shape=jax.ShapeDtypeStruct((PIECES, PIECE, 128), BF16),
        interpret=INTERPRET,
        name="pair_add",
    )(a, b)


def sum_kernel(a, o, acc):
    i = pl.program_id(0)

    @pl.when(i == 0)
    def _():
        acc[...] = jnp.zeros_like(acc)

    acc[...] += jnp.sum(a[...].astype(F32), axis=0)

    @pl.when(i == pl.num_programs(0) - 1)
    def _():
        o[:DATA, :] = acc[:DATA, :].astype(BF16)
        o[DATA:, :] = resplit(acc[DATA:, :]).astype(BF16)


def chip_sum(a):
    return pl.pallas_call(
        sum_kernel,
        grid=(PIECES // 16,),
        in_specs=[pl.BlockSpec((16, PIECE, 128), lambda i: (i, 0, 0))],
        out_specs=pl.BlockSpec((PIECE, 128), lambda i: (0, 0)),
        out_shape=jax.ShapeDtypeStruct((PIECE, 128), BF16),
        scratch_shapes=[pltpu.VMEM((PIECE, 128), F32)],
        interpret=INTERPRET,
        name="chip_sum",
    )(a)


def finish_kernel(g0, g1, tail, dx, gin, gout, gtok, gbias, loss):
    last = tail[DATA:, :].astype(F32)
    last = last[0:1, :] + last[2:3, :] + last[4:5, :]
    total = last[0:1, 1:2]
    i = pl.program_id(0)

    @pl.when(i == 0)
    def _():
        loss[...] = jnp.broadcast_to(last[0:1, 0:1] / total, (8, 128))

    def piece(p, carry):
        rows = pl.ds(pl.multiple_of(p * 16, 16), 16)
        for j in range(2 * BLOCKS):
            g = (g0, g1)[j // BLOCKS]
            jj = j % BLOCKS
            value = (g[p, jj * 16 : (jj + 1) * 16, :].astype(F32) / total).astype(BF16)
            if j < 20:
                gin[rows, j * 128 : (j + 1) * 128] = value
            else:
                gout[rows, (j - 20) * 128 : (j - 19) * 128] = value
        return carry

    lax.fori_loop(0, 8, piece, 0)
    gtok[...] = (dx[...] / total).astype(BF16)
    e = g0[:, DATA:, :].astype(F32)
    gbias[...] = (e[:, 0:2, :] + e[:, 2:4, :] + e[:, 4:6, :]) / total


def finish(gathered, dx):
    return pl.pallas_call(
        finish_kernel,
        grid=(8,),
        in_specs=[
            pl.BlockSpec((8, None, PIECE, 128), lambda i: (i, 0, 0, 0)),
            pl.BlockSpec((8, None, PIECE, 128), lambda i: (i, 1, 0, 0)),
            pl.BlockSpec((None, None, PIECE, 128), lambda i: (10, 0, 0, 0)),
            pl.BlockSpec((64, D), lambda i: (i, 0)),
        ],
        out_specs=[
            pl.BlockSpec((128, COLS), lambda i: (i, 0)),
            pl.BlockSpec((128, D), lambda i: (i, 0)),
            pl.BlockSpec((64, D), lambda i: (i, 0)),
            pl.BlockSpec((8, 2, 128), lambda i: (i, 0, 0)),
            pl.BlockSpec((8, 128), lambda i: (0, 0)),
        ],
        out_shape=[
            jax.ShapeDtypeStruct((D, COLS), BF16),
            jax.ShapeDtypeStruct((D, D), BF16),
            jax.ShapeDtypeStruct((ROWS, D), BF16),
            jax.ShapeDtypeStruct((PIECES, 2, 128), F32),
            jax.ShapeDtypeStruct((8, 128), F32),
        ],
        interpret=INTERPRET,
        name="finish",
    )(gathered, gathered, gathered, dx)


def shards(tokens, labels, lengths, targets, w_in, b_in, w_out):
    core = lax.axis_index("c").astype(jnp.int32)
    meta = jnp.concatenate([lengths, core[None]])
    out, dx, mine, send = local_step(
        meta, targets.reshape(4, 128), tokens, labels, w_in, b_in.reshape(1, COLS), w_out
    )
    other = lax.ppermute(send, "c", [(0, 1), (1, 0)])
    both = pair_add(mine, other)
    spread = lax.all_to_all(both, CHIPS, 0, 0, tiled=True)
    piece = chip_sum(spread)
    gathered = lax.all_gather(piece, AXES, axis=0, tiled=False).reshape(PIECES, 2, PIECE, 128)
    gin, gout, gtok, gbias, loss = finish(gathered, dx)
    return out, loss[0, 0], gtok, gin, gbias[:10].reshape(COLS), gout


def solution(mesh):
    torus = Mesh(mesh.devices.reshape(4, 4, 4, 2), AXES)
    placed = (P(AXES, None), P(AXES, None), P(AXES), P(AXES), P(), P(), P())
    return jax.shard_map(
        shards,
        mesh=torus,
        in_specs=placed,
        out_specs=(P(AXES, None), P(), P(AXES, None), P(), P(), P()),
        check_vma=False,
    )
```

time: 272 us -> 210 us (0.77)
  Pallas kernels: 0 us -> 56.7 us
  matrix products: 42.8 us -> 0 us
  other arithmetic: 31.3 us -> 1.24 us
  waiting for transfers between devices: 99.2 us -> 74.5 us
  local copies, waits for them, and re-layouts: 19.4 us -> 3.83 us
  blocking collectives: 61.6 us -> 57.9 us
  between operations: 16.8 us -> 14 us
    psum x1 -> x0, waiting for transfers between devices: 99.1 us -> none  [shards(): sum_in, sum_out = lax.psum((d_in, d_out), BLK)]
    all_gather x0 -> x1, waiting for transfers between devices: none -> 67.9 us  [shards(): lax.all_gather(piece, AXES, axis=0, tiled=False)]
    psum x4 -> x0, blocking collectives: 61.6 us -> none  [one_axis_at_a_time(): return functools.reduce(lax.psum, axes, x)]
    all_to_all x0 -> x1, blocking collectives: none -> 57.9 us  [shards(): spread = lax.all_to_all(both, CHIPS, 0, 0, tiled=True)]
    pallas_call x0 -> x4, Pallas kernels: none -> 56.7 us  [the longest x1 32.8 us: local_step(): pl.pallas_call(local_kernel, in_specs=[pl.BlockSpec(memory_space=pltpu.SM...]
    dot_general x12 -> x0, matrix products: 42.8 us -> none  [the longest x3 19.4 us: history_layer(): hidden = jnp.dot(normed, w_in, preferred_element_type=jnp.float32) + b_in]
    convert_element_type x3 -> x0, other arithmetic: 14 us -> none  [the longest x1 8.62 us: shards(): grad_in = (sum_in / total).astype(jnp.bfloat16)]
    reduce_sum x7 -> x0, other arithmetic: 12 us -> none  [the longest x3 4.54 us: norm_rows(): center = values - jnp.mean(values, axis=-1, keepdims=True)]
  transfers between devices with their start and end apart: 1 -> 2, of which waited for: 1 -> 2; matrix products, arithmetic and copies ran while one was open for 6% -> 0% of each run, Pallas kernels for 0% -> 0%
where the time goes in v1:
time: 210 us
  waiting for transfers between devices  74.5 us (35%)
  blocking collectives  57.9 us (28%)
  Pallas kernels  56.7 us (27%)
  between operations  14 us (7%)
  local copies, waits for them, and re-layouts  3.83 us (2%)
    all_gather x1, waiting for transfers between devices, shards(): lax.all_gather(piece, AXES, axis=0, tiled=False)  67.9 us
    all_to_all x1, blocking collectives, shards(): spread = lax.all_to_all(both, CHIPS, 0, 0, tiled=True)  57.9 us
    pallas_call x1, Pallas kernels, local_step(): pl.pallas_call(local_kernel, in_specs=[pl.BlockSpec(memory_space=pltpu.SM...  32.8 us
    pallas_call x1, Pallas kernels, finish(): pl.pallas_call(finish_kernel, grid=(8,), in_specs=[pl.BlockSpec((8, None,...  12.7 us
    pallas_call x1, Pallas kernels, pair_add(): pl.pallas_call(pair_kernel, grid=(PIECES // 8,), in_specs=[spec, spec], o...  7.5 us
    ppermute x1, waiting for transfers between devices, shards(): other = lax.ppermute(send, 'c', [(0, 1), (1, 0)])  6.57 us
  transfers between devices with their start and end apart: 2, of which 2 were waited for; matrix products, arithmetic and copies ran while one was open for 0% of the time, Pallas kernels for 0%

profile of v1, /device:TPU:1, one launch (start us, length us, event | category | flops | bytes accessed | tf_op | source)
XLA Modules:
  0.0 209.7 jit_solution(2040839377105745592)
XLA Ops:
  7.2 0.0 all-gather.3.cloned.1.call-start
  7.2 1.3 reshape.25.bias
  8.5 1.2 pad_add_fusion.meta
  9.8 32.8 %local_step.1 = (bf16[512,1024]{1,0:T(8,128)(2,1)}, f32[512,1024]{1,0:T(8,128)}, bf16[64,232,128]{2,1,0:T(8,128)(2,1)}, bf16[64,232,128]{2,1,0:T(8,128)(2,1)}) custom-call(s32[3]{0:T(128)} %pad_add_fusion.meta, s32[4,128]{1,0:T(4,128)} %bitcast.9, bf16[512,1024]{1,0:T(8,128)(2,1)} %tok.1, bf16[512,1024]{1,0:T(8,128)(2,1)} %lab.1, bf16[1024,2560]{1,0:T(8,128)(2,1)} %win.1, ...), custom_call_target="tpu_custom_call" | custom-call | tf_op jit(solution)/shard_map/local_step/pallas_call | solution.py:230
  42.6 1.5 collective-permute-start
  44.1 6.6 %collective-permute-done.b = bf16[64,232,128]{2,1,0:T(8,128)(2,1)} collective-permute-done((bf16[64,232,128]{2,1,0:T(8,128)(2,1)}, bf16[64,232,128]{2,1,0:T(8,128)(2,1)}, u32[]{:S(2)}, u32[]{:S(2)}) %collective-permute-start) | collective-permute-done | bytes 3801120 | tf_op jit(solution)/shard_map/ppermute | solution.py:382
  50.6 7.5 %pair_add.1 = bf16[64,232,128]{2,1,0:T(8,128)(2,1)} custom-call(bf16[64,232,128]{2,1,0:T(8,128)(2,1)} %get-tuple-element.16.a, bf16[64,232,128]{2,1,0:T(8,128)(2,1)} %collective-permute-done.b), custom_call_target="tpu_custom_call" | custom-call | tf_op jit(solution)/shard_map/pair_add/pallas_call | solution.py:280
  58.2 57.9 %all_to_all.5.a = bf16[64,232,128]{2,1,0:T(8,128)(2,1)} all-to-all(bf16[64,232,128]{2,1,0:T(8,128)(2,1)} %pair_add.1), channel_id=1, replica_groups=mesh['z'=4,'x'=4,'y'=4,'c'=2] {'z','x','y'}, dimensions={0} | all-to-all | bytes 7602176 | tf_op jit(solution)/shard_map/all_to_all | solution.py:384
  116.1 3.7 %chip_sum.1 = bf16[232,128]{1,0:T(8,128)(2,1)} custom-call(bf16[64,232,128]{2,1,0:T(8,128)(2,1)} %all_to_all.5.a), custom_call_target="tpu_custom_call" | custom-call | tf_op jit(solution)/shard_map/chip_sum/pallas_call | solution.py:307
  119.7 0.0 all-gather.3.cloned.1.call-update
  119.8 67.9 %all-gather.3.cloned.1.call-done = bf16[29696,128]{1,0:T(8,128)(2,1)} async-done(((bf16[232,128]{1,0:T(8,128)(2,1)}), bf16[29696,128]{1,0:T(8,128)(2,1)}) %all-gather.3.cloned.1.call-update) | async-done | bytes 7602192 | tf_op jit(solution)/shard_map/all_gather | solution.py:386
  187.7 12.7 %finish.1 = (bf16[1024,2560]{1,0:T(8,128)(2,1)}, bf16[1024,1024]{1,0:T(8,128)(2,1)}, bf16[512,1024]{1,0:T(8,128)(2,1)}, f32[64,2,128]{2,1,0:T(2,128)}, f32[8,128]{1,0:T(8,128)}) custom-call(bf16[64,2,232,128]{3,2,1,0:T(8,128)(2,1)} %bitcast.6, bf16[64,2,232,128]{3,2,1,0:T(8,128)(2,1)} %bitcast.7, bf16[64,2,232,128]{3,2,1,0:T(8,128)(2,1)} %bitcast.8, ...), custom_call_target="tpu_custom_call" | custom-call | tf_op jit(solution)/shard_map/finish/pallas_call | solution.py:348
  200.3 1.2 slice.6
  201.5 0.7 slice.7
  202.2 0.6 reshape.27
Async XLA Ops:
  7.2 180.5 %all-gather.3.cloned.1.call-start = ((), (), s32[]{:S(2)}) async-start(), calls=%async_computation.1 | async-start | bytes 7661568 | tf_op jit(solution)/shard_map/all_gather | solution.py:386
  42.6 8.0 %collective-permute-start = (bf16[64,232,128]{2,1,0:T(8,128)(2,1)}, bf16[64,232,128]{2,1,0:T(8,128)(2,1)}, u32[]{:S(2)}, u32[]{:S(2)}) collective-permute-start(bf16[64,232,128]{2,1,0:T(8,128)(2,1)} %get-tuple-element.17), channel_id=1, source_target_pairs={{0,1},{1,0},{2,3},{3,2},{4,5},{5,4},{6,7},{7,6},{8,9},{9,8},{10,11... | collective-permute-start | bytes 11403272 | tf_op jit(solution)/shard_map/ppermute | solution.py:382
Sparse Core Ops, SparseCore 0:
  119.9 67.7 all-gather.2

commit v2 on v1

v2 whole, which is shorter than its diff:
```python
import functools

import jax
import jax.numpy as jnp
from jax import lax
from jax.experimental import pallas as pl
from jax.experimental.pallas import tpu as pltpu
from jax.sharding import Mesh
from jax.sharding import PartitionSpec as P

D = 1024
HEADS = 4
VDIM = 256
QKDIM = 64
LMAX = 256
COLS = 2560
REST = 1536
ROWS = 512
QCOL = 1024
KCOL = 1280
AXES = ("z", "x", "y", "c")
CHIPS = ("z", "x", "y")
PIECES = 64
BLOCKS_A = 8
BLOCKS_B = 6
PIECE_A = BLOCKS_A * 16 + 8
PIECE_B = BLOCKS_B * 16 + 8
EPS = 1e-05
F32 = jnp.float32
BF16 = jnp.bfloat16
VM = pl.BlockSpec(memory_space=pltpu.VMEM)
SM = pl.BlockSpec(memory_space=pltpu.SMEM)
HBM = pl.BlockSpec(memory_space=pl.ANY)


def cost(flops):
    return pl.CostEstimate(flops=flops, transcendentals=0, bytes_accessed=8 * 2**20)


def sigmoid(h):
    return 0.5 * jnp.tanh(0.5 * h) + 0.5


def silu_slope(h, sg):
    return sg * (1.0 + h * (1.0 - sg))


def nn(a, b):
    return jnp.dot(a, b, preferred_element_type=F32)


def nt(a, b):
    return lax.dot_general(a, b, (((1,), (1,)), ((), ())), preferred_element_type=F32)


def tn(a, b):
    return lax.dot_general(a, b, (((0,), (0,)), ((), ())), preferred_element_type=F32)


def three_parts(value):
    hi = value.astype(BF16).astype(F32)
    rest = value - hi
    mid = rest.astype(BF16).astype(F32)
    low = (rest - mid).astype(BF16).astype(F32)
    return hi, mid, low


def row_stats(x):
    center = x - jnp.mean(x, axis=-1, keepdims=True)
    spread = jnp.mean(center * center, axis=-1, keepdims=True)
    return center, lax.rsqrt(spread + EPS)


def allowed_mask(length):
    i = lax.broadcasted_iota(jnp.int32, (LMAX, LMAX), 0)
    j = lax.broadcasted_iota(jnp.int32, (LMAX, LMAX), 1)
    return (j <= i) & (j < length)


def wide_row(ref, first, count):
    return jnp.concatenate([ref[j : j + 1, :] for j in range(first, first + count)], axis=1)


def pack(pay, blocks, j, value):
    half, jj = j // blocks, j % blocks
    pay[half, :, jj * 16 : (jj + 1) * 16, :] = value.astype(BF16).reshape(PIECES, 16, 128)


def forward_kernel(
    lens, tgt, tok, lab, win_hbm, bias, wout_hbm,
    out, mine, send, normed_t_out, acts_out, slope_out, dm_out, cot_out, dhu_out, bsum,
    win, wout, normed, normed_t, gate_h, gate_a, acts, slope, mixed, gated_t, dm, cot, dhu, lsum, csum, pay, sems,
):
    core = lax.axis_index("c")
    load_in = pltpu.make_async_copy(win_hbm, win, sems.at[0])
    load_out = pltpu.make_async_copy(wout_hbm, wout, sems.at[1])
    load_in.start()
    load_out.start()
    bsum[...] = jnp.zeros_like(bsum)
    lsum[...] = jnp.zeros_like(lsum)
    csum[...] = jnp.zeros_like(csum)
    lane = lax.broadcasted_iota(jnp.int32, (8, 128), 1)
    line = lax.broadcasted_iota(jnp.int32, (8, 128), 0)

    def prologue(r, carry):
        rows = pl.ds(pl.multiple_of(r * 128, 128), 128)
        length = lens[r // 2]
        place = (r % 2) * 128 + lax.broadcasted_iota(jnp.int32, (128, 128), 0)
        marks = jnp.transpose(jnp.broadcast_to(tgt[pl.ds(r, 1), :].astype(F32), (128, 128)))
        chosen = ((marks == 1.0) | (place == length - 1)) & (place < length)
        flag = jnp.where(chosen, 1.0, 0.0)
        csum[...] += jnp.sum(flag, axis=0, keepdims=True)
        wide = jnp.concatenate([flag] * 8, axis=1)
        cot[rows, :] = jnp.where(wide > 0.0, lab[rows, :].astype(F32), 0.0).astype(BF16)
        center, inv = row_stats(tok[rows, :].astype(F32))
        y = center * inv
        normed[rows, :] = y.astype(BF16)
        normed_t[:, rows] = jnp.transpose(y).astype(BF16)
        return carry

    lax.fori_loop(0, 4, prologue, 0)
    save_nt = pltpu.make_async_copy(normed_t, normed_t_out, sems.at[2])
    save_cot = pltpu.make_async_copy(cot, cot_out, sems.at[3])
    save_nt.start()
    save_cot.start()
    load_in.wait()

    for c in range(5):
        h = nn(normed[...], win[:, c * 512 : (c + 1) * 512]) + wide_row(bias, 4 * c, 4)
        sg = sigmoid(h)
        if c < 2:
            gate_h[:, c * 512 : (c + 1) * 512] = silu_slope(h, sg).astype(BF16)
            gate_a[:, c * 512 : (c + 1) * 512] = (h * sg).astype(BF16)
        else:
            slope[:, (c - 2) * 512 : (c - 1) * 512] = silu_slope(h, sg).astype(BF16)
            acts[:, (c - 2) * 512 : (c - 1) * 512] = (h * sg).astype(BF16)
    save_acts = pltpu.make_async_copy(acts, acts_out, sems.at[4])
    save_slope = pltpu.make_async_copy(slope, slope_out, sems.at[5])
    save_acts.start()
    save_slope.start()

    for n in range(2):
        rows = slice(n * LMAX, (n + 1) * LMAX)
        allowed = allowed_mask(lens[n])
        for h in range(HEADS):
            q = acts[rows, QCOL + h * QKDIM : QCOL + (h + 1) * QKDIM]
            k = acts[rows, KCOL + h * QKDIM : KCOL + (h + 1) * QKDIM]
            s = nt(q, k)
            w = jnp.where(allowed, s * sigmoid(s), 0.0).astype(BF16)
            mixed[rows, h * VDIM : (h + 1) * VDIM] = nn(w, acts[rows, h * VDIM : (h + 1) * VDIM])

    load_out.wait()

    def gate(r, carry):
        rows = pl.ds(pl.multiple_of(r * 128, 128), 128)
        center, inv = row_stats(mixed[rows, :])
        y = center * inv
        u = gate_a[rows, :].astype(F32)
        gated = (y * u).astype(BF16)
        gated_t[:, rows] = jnp.transpose(gated.astype(F32)).astype(BF16)
        length = lens[r // 2]
        place = (r % 2) * 128 + lax.broadcasted_iota(jnp.int32, (128, D), 0)
        full = tok[rows, :].astype(F32) + nn(gated, wout[...])
        rounded = jnp.where(place < length, full, 0.0).astype(BF16)
        out[rows, :] = rounded
        c = cot[rows, :]
        lsum[...] += jnp.sum(c.astype(F32) * rounded.astype(F32), axis=0, keepdims=True)
        dg = nt(c, wout[...]).astype(BF16).astype(F32)
        dy = dg * u
        du = (dg * y).astype(BF16).astype(F32)
        m1 = jnp.mean(dy, axis=-1, keepdims=True)
        m2 = jnp.mean(dy * y, axis=-1, keepdims=True)
        dm[rows, :] = (inv * (dy - m1 - y * m2)).astype(BF16)
        dh = du * gate_h[rows, :].astype(F32)
        dhu[rows, :] = dh.astype(BF16)
        bsum[0:1, :] += jnp.sum(dh, axis=0, keepdims=True)
        return carry

    lax.fori_loop(0, 4, gate, 0)
    save_dm = pltpu.make_async_copy(dm, dm_out, sems.at[6])
    save_dhu = pltpu.make_async_copy(dhu, dhu_out, sems.at[7])
    save_dm.start()
    save_dhu.start()

    for c in range(2):
        g = nn(gated_t[...], cot[:, c * 512 : (c + 1) * 512])
        for i in range(4):
            pack(pay, BLOCKS_A, 4 * c + i, g[:, i * 128 : (i + 1) * 128])
    for c in range(2):
        g = nn(normed_t[...], dhu[:, c * 512 : (c + 1) * 512])
        for i in range(4):
            pack(pay, BLOCKS_A, 8 + 4 * c + i, g[:, i * 128 : (i + 1) * 128])

    loss = jnp.sum(lsum[...], axis=1, keepdims=True)
    tail = jnp.where(lane == 0, jnp.broadcast_to(loss, (8, 128)), 0.0)
    tail = jnp.where(lane == 1, jnp.broadcast_to(csum[...], (8, 128)), tail)
    hi, mid, low = three_parts(tail)
    ext = jnp.where(line == 0, hi, jnp.where(line == 2, mid, jnp.where(line == 4, low, 0.0)))
    for half in range(2):
        pay[half, :, BLOCKS_A * 16 :, :] = jnp.zeros((PIECES, 8, 128), BF16)
        pay[half, 0, BLOCKS_A * 16 :, :] = ext.astype(BF16)

    to_send = pltpu.make_async_copy(pay.at[1 - core], send, sems.at[8])
    to_keep = pltpu.make_async_copy(pay.at[core], mine, sems.at[9])
    to_send.start()
    to_keep.start()
    for copy in (save_nt, save_cot, save_acts, save_slope, save_dm, save_dhu, to_send, to_keep):
        copy.wait()


def forward_step(lens, tgt, tok, lab, win, bias, wout):
    half = jax.ShapeDtypeStruct((PIECES, PIECE_A, 128), BF16)
    saved = [(D, ROWS), (ROWS, REST), (ROWS, REST), (ROWS, D), (ROWS, D), (ROWS, D)]
    return pl.pallas_call(
        forward_kernel,
        in_specs=[SM, VM, VM, VM, HBM, VM, HBM],
        out_specs=[VM] + [HBM] * 8 + [VM],
        out_shape=[jax.ShapeDtypeStruct((ROWS, D), BF16), half, half]
        + [jax.ShapeDtypeStruct(s, BF16) for s in saved]
        + [jax.ShapeDtypeStruct((1, D), F32)],
        scratch_shapes=[
            pltpu.VMEM((D, COLS), BF16),
            pltpu.VMEM((D, D), BF16),
            pltpu.VMEM((ROWS, D), BF16),
            pltpu.VMEM((D, ROWS), BF16),
            pltpu.VMEM((ROWS, D), BF16),
            pltpu.VMEM((ROWS, D), BF16),
            pltpu.VMEM((ROWS, REST), BF16),
            pltpu.VMEM((ROWS, REST), BF16),
            pltpu.VMEM((ROWS, D), F32),
            pltpu.VMEM((D, ROWS), BF16),
            pltpu.VMEM((ROWS, D), BF16),
            pltpu.VMEM((ROWS, D), BF16),
            pltpu.VMEM((ROWS, D), BF16),
            pltpu.VMEM((1, D), F32),
            pltpu.VMEM((1, 128), F32),
            pltpu.VMEM((2, PIECES, PIECE_A, 128), BF16),
            pltpu.SemaphoreType.DMA((10,)),
        ],
        compiler_params=pltpu.CompilerParams(vmem_limit_bytes=48 * 2**20),
        cost_estimate=cost(16 * 10**9),
        name="forward_step",
    )(lens, tgt, tok, lab, win, bias, wout)


def attention_kernel(lens, acts, slope, dm, dh, bsum, dqk):
    bsum[...] = jnp.zeros_like(bsum)
    for n in range(2):
        rows = slice(n * LMAX, (n + 1) * LMAX)
        allowed = allowed_mask(lens[n])
        for h in range(HEADS):
            q = acts[rows, QCOL + h * QKDIM : QCOL + (h + 1) * QKDIM]
            k = acts[rows, KCOL + h * QKDIM : KCOL + (h + 1) * QKDIM]
            vc = slice(h * VDIM, (h + 1) * VDIM)
            d = dm[rows, vc]
            s = nt(q, k)
            sg = sigmoid(s)
            w = jnp.where(allowed, s * sg, 0.0).astype(BF16)
            dw = nt(d, acts[rows, vc]).astype(BF16).astype(F32)
            dv = tn(w, d).astype(BF16).astype(F32)
            ds = jnp.where(allowed, dw * silu_slope(s, sg), 0.0).astype(BF16)
            dqk[rows, h * QKDIM : (h + 1) * QKDIM] = nn(ds, k)
            dqk[rows, 256 + h * QKDIM : 256 + (h + 1) * QKDIM] = tn(ds, q)
            dhv = dv * slope[rows, vc].astype(F32)
            dh[rows, vc] = dhv.astype(BF16)
            bsum[0:1, vc] += jnp.sum(dhv, axis=0, keepdims=True)
        dhq = dqk[rows, :].astype(BF16).astype(F32) * slope[rows, QCOL:].astype(F32)
        dh[rows, QCOL:] = dhq.astype(BF16)
        bsum[0:1, QCOL:] += jnp.sum(dhq, axis=0, keepdims=True)


def attention_back(lens, acts, slope, dm):
    return pl.pallas_call(
        attention_kernel,
        in_specs=[SM, VM, VM, VM],
        out_specs=[VM, VM],
        out_shape=[jax.ShapeDtypeStruct((ROWS, REST), BF16), jax.ShapeDtypeStruct((1, REST), F32)],
        scratch_shapes=[pltpu.VMEM((ROWS, 512), F32)],
        cost_estimate=cost(6 * 10**9),
        name="attention_back",
    )(lens, acts, slope, dm)


def weights_kernel(normed_t, dh, bsum_u, bsum_r, after, mine, send, pay, ext, sems):
    core = lax.axis_index("c")
    for c in range(3):
        g = nn(normed_t[...], dh[:, c * 512 : (c + 1) * 512])
        for i in range(4):
            pack(pay, BLOCKS_B, 4 * c + i, g[:, i * 128 : (i + 1) * 128])
    ext[...] = jnp.zeros_like(ext)
    for j in range(COLS // 128):
        row = bsum_u[0:1, j * 128 : (j + 1) * 128] if j < 8 else bsum_r[0:1, (j - 8) * 128 : (j - 7) * 128]
        parts = three_parts(row)
        base = 8 * (j // 2) + j % 2
        for t in range(3):
            ext[base + 2 * t : base + 2 * t + 1, :] = parts[t]
    for half in range(2):
        pay[half, :, BLOCKS_B * 16 :, :] = jnp.zeros((PIECES, 8, 128), BF16)
        for p in range(10):
            pay[half, p, BLOCKS_B * 16 :, :] = ext[8 * p : 8 * p + 8, :].astype(BF16)
    to_send = pltpu.make_async_copy(pay.at[1 - core], send, sems.at[0])
    to_keep = pltpu.make_async_copy(pay.at[core], mine, sems.at[1])
    to_send.start()
    to_keep.start()
    to_send.wait()
    to_keep.wait()


def weights_step(normed_t, dh, bsum_u, bsum_r, after):
    half = jax.ShapeDtypeStruct((PIECES, PIECE_B, 128), BF16)
    return pl.pallas_call(
        weights_kernel,
        in_specs=[VM, VM, VM, VM, HBM],
        out_specs=[HBM, HBM],
        out_shape=[half, half],
        scratch_shapes=[
            pltpu.VMEM((2, PIECES, PIECE_B, 128), BF16),
            pltpu.VMEM((80, 128), F32),
            pltpu.SemaphoreType.DMA((2,)),
        ],
        cost_estimate=cost(4 * 10**9),
        name="weights_step",
    )(normed_t, dh, bsum_u, bsum_r, after)


def rows_kernel(dhu, dhr, win, tok, cot, after, dx, acc):
    i = pl.program_id(0)

    @pl.when(i == 0)
    def _():
        acc[...] = nt(dhu[...], win[...])

    @pl.when((i > 0) & (i < 2))
    def _():
        acc[...] += nt(dhu[...], win[...])

    @pl.when(i >= 2)
    def _():
        acc[...] += nt(dhr[...], win[...])

    @pl.when(i == 4)
    def _():
        def back(r, carry):
            rows = pl.ds(pl.multiple_of(r * 128, 128), 128)
            dn = acc[rows, :].astype(BF16).astype(F32)
            center, inv = row_stats(tok[rows, :].astype(F32))
            y = center * inv
            m1 = jnp.mean(dn, axis=-1, keepdims=True)
            m2 = jnp.mean(dn * y, axis=-1, keepdims=True)
            dx[rows, :] = inv * (dn - m1 - y * m2) + cot[rows, :].astype(F32)
            return carry

        lax.fori_loop(0, 4, back, 0)


def rows_step(dhu, dhr, win, tok, cot, after):
    whole = pl.BlockSpec((ROWS, D), lambda i: (0, 0))
    return pl.pallas_call(
        rows_kernel,
        grid=(5,),
        in_specs=[
            pl.BlockSpec((ROWS, 512), lambda i: (0, jnp.minimum(i, 1))),
            pl.BlockSpec((ROWS, 512), lambda i: (0, jnp.maximum(i - 2, 0))),
            pl.BlockSpec((D, 512), lambda i: (0, i)),
            whole,
            whole,
            HBM,
        ],
        out_specs=whole,
        out_shape=jax.ShapeDtypeStruct((ROWS, D), F32),
        scratch_shapes=[pltpu.VMEM((ROWS, D), F32)],
        cost_estimate=cost(6 * 10**9),
        name="rows_step",
    )(dhu, dhr, win, tok, cot, after)


def resplit(total):
    value = total[..., 0:2, :] + total[..., 2:4, :] + total[..., 4:6, :]
    hi, mid, low = three_parts(value)
    return jnp.concatenate([hi, mid, low, jnp.zeros_like(hi)], axis=-2)


def pair_kernel(a, b, o):
    data = a.shape[1] - 8
    o[:, :data, :] = (a[:, :data, :].astype(F32) + b[:, :data, :].astype(F32)).astype(BF16)
    o[:, data:, :] = resplit(a[:, data:, :].astype(F32) + b[:, data:, :].astype(F32)).astype(BF16)


def pair_add(a, b):
    spec = pl.BlockSpec((16,) + a.shape[1:], lambda i: (i, 0, 0))
    return pl.pallas_call(
        pair_kernel,
        grid=(PIECES // 16,),
        in_specs=[spec, spec],
        out_specs=spec,
        out_shape=jax.ShapeDtypeStruct(a.shape, BF16),
        cost_estimate=cost(2 * 10**9),
        name="pair_add",
    )(a, b)


def sum_kernel(a, o, acc, piece, sem):
    i = pl.program_id(0)
    data = a.shape[1] - 8

    @pl.when(i == 0)
    def _():
        acc[...] = jnp.zeros_like(acc)

    acc[...] += jnp.sum(a[...].astype(F32), axis=0)

    @pl.when(i == pl.num_programs(0) - 1)
    def _():
        piece[:data, :] = acc[:data, :].astype(BF16)
        piece[data:, :] = resplit(acc[data:, :]).astype(BF16)
        copies = [pltpu.make_async_copy(piece, o.at[p], sem.at[p]) for p in range(PIECES)]
        for copy in copies:
            copy.start()
        for copy in copies:
            copy.wait()


def chip_sum(a):
    _, size, _ = a.shape
    return pl.pallas_call(
        sum_kernel,
        grid=(PIECES // 16,),
        in_specs=[pl.BlockSpec((16, size, 128), lambda i: (i, 0, 0))],
        out_specs=HBM,
        out_shape=jax.ShapeDtypeStruct(a.shape, BF16),
        scratch_shapes=[
            pltpu.VMEM((size, 128), F32),
            pltpu.VMEM((size, 128), BF16),
            pltpu.SemaphoreType.DMA((PIECES,)),
        ],
        cost_estimate=cost(2 * 10**9),
        name="chip_sum",
    )(a)


def finish_a_kernel(own, other, tail, dx, gin, gout, gtok, scale, loss):
    core = lax.axis_index("c")
    last = tail[BLOCKS_A * 16 :, :].astype(F32)
    last = last[0:1, :] + last[2:3, :] + last[4:5, :]
    inverse = 1.0 / last[0:1, 1:2]
    scale[...] = jnp.broadcast_to(inverse, (8, 128))
    loss[...] = last[0:1, 0:1] * inverse

    def move(src, dst):
        def piece(p, carry):
            rows = pl.ds(pl.multiple_of(p * 16, 16), 16)
            for j in range(BLOCKS_A):
                value = src[p, j * 16 : (j + 1) * 16, :].astype(F32) * inverse
                dst[rows, j * 128 : (j + 1) * 128] = value.astype(BF16)
            return carry

        lax.fori_loop(0, 16, piece, 0)

    @pl.when(core == 0)
    def _():
        move(own, gout)
        move(other, gin)

    @pl.when(core == 1)
    def _():
        move(other, gout)
        move(own, gin)

    gtok[...] = (dx[...] * inverse).astype(BF16)


def finish_a(own, other, dx):
    spec = pl.BlockSpec((16, PIECE_A, 128), lambda i: (i, 0, 0))
    return pl.pallas_call(
        finish_a_kernel,
        grid=(4,),
        in_specs=[spec, spec, pl.BlockSpec((None, PIECE_A, 128), lambda i: (0, 0, 0)), pl.BlockSpec((128, D), lambda i: (i, 0))],
        out_specs=[
            pl.BlockSpec((256, D), lambda i: (i, 0)),
            pl.BlockSpec((256, D), lambda i: (i, 0)),
            pl.BlockSpec((128, D), lambda i: (i, 0)),
            pl.BlockSpec((8, 128), lambda i: (0, 0)),
            pl.BlockSpec((1, 1), lambda i: (0, 0)),
        ],
        out_shape=[
            jax.ShapeDtypeStruct((D, COLS), BF16),
            jax.ShapeDtypeStruct((D, D), BF16),
            jax.ShapeDtypeStruct((ROWS, D), BF16),
            jax.ShapeDtypeStruct((8, 128), F32),
            jax.ShapeDtypeStruct((1, 1), F32),
        ],
        cost_estimate=cost(3 * 10**9),
        name="finish_a",
    )(own, other, own, dx)


def finish_b_kernel(own, other, tail, scale, gin_in, gin, gbias, buf, sems):
    core = lax.axis_index("c")
    i = pl.program_id(0)
    inverse = scale[0:1, 0:1]

    def move(src, first):
        def piece(p, carry):
            rows = pl.ds(pl.multiple_of(p * 16, 16), 16)
            for j in range(BLOCKS_B):
                value = src[p, j * 16 : (j + 1) * 16, :].astype(F32) * inverse
                buf[i, rows, (first + j) * 128 : (first + j + 1) * 128] = value.astype(BF16)
            return carry

        lax.fori_loop(0, 16, piece, 0)

    @pl.when(core == 0)
    def _():
        move(own, 0)
        move(other, BLOCKS_B)

    @pl.when(core == 1)
    def _():
        move(other, 0)
        move(own, BLOCKS_B)

    def save(t):
        return pltpu.make_async_copy(buf.at[t], gin.at[pl.ds(t * 256, 256), pl.ds(D, REST)], sems.at[t])

    save(i).start()

    @pl.when(i == 0)
    def _():
        for p in range(10):
            e = tail[p, BLOCKS_B * 16 :, :].astype(F32)
            gbias[2 * p : 2 * p + 2, :] = (e[0:2, :] + e[2:4, :] + e[4:6, :]) * inverse

    @pl.when(i == 3)
    def _():
        for t in range(4):
            save(t).wait()


def finish_b(own, other, scale, gin):
    spec = pl.BlockSpec((16, PIECE_B, 128), lambda i: (i, 0, 0))
    return pl.pallas_call(
        finish_b_kernel,
        grid=(4,),
        in_specs=[
            spec,
            spec,
            pl.BlockSpec((16, PIECE_B, 128), lambda i: (0, 0, 0)),
            pl.BlockSpec((8, 128), lambda i: (0, 0)),
            HBM,
        ],
        out_specs=[HBM, pl.BlockSpec((20, 128), lambda i: (0, 0))],
        out_shape=[jax.ShapeDtypeStruct((D, COLS), BF16), jax.ShapeDtypeStruct((20, 128), F32)],
        input_output_aliases={4: 0},
        scratch_shapes=[pltpu.VMEM((4, 256, REST), BF16), pltpu.SemaphoreType.DMA((4,))],
        cost_estimate=cost(3 * 10**9),
        name="finish_b",
    )(own, other, own, scale, gin)


def swap(value):
    return lax.ppermute(value, "c", [(0, 1), (1, 0)])


def exchange(value):
    return lax.all_to_all(value, CHIPS, 0, 0, tiled=True)


def shards(tokens, labels, lengths, targets, w_in, b_in, w_out):
    out, mine_a, send_a, normed_t, acts, slope, dm, cot, dhu, bsum_u = forward_step(
        lengths, targets.reshape(4, 128), tokens, labels, w_in, b_in.reshape(20, 128), w_out
    )
    other_a = swap(send_a)
    dhr, bsum_r = attention_back(lengths, acts, slope, dm)
    pair_a = pair_add(mine_a, other_a)
    spread_a = exchange(pair_a)
    mine_b, send_b = weights_step(normed_t, dhr, bsum_u, bsum_r, pair_a)
    other_b = swap(send_b)
    dx = rows_step(dhu, dhr, w_in, tokens, cot, mine_b)
    pair_b = pair_add(mine_b, other_b)
    spread_b = exchange(pair_b)
    copies_a = chip_sum(spread_a)
    own_a = exchange(copies_a)
    copies_b = chip_sum(spread_b)
    own_b = exchange(copies_b)
    gin, gout, gtok, scale, loss = finish_a(own_a, swap(own_a), dx)
    gin, gbias = finish_b(own_b, swap(own_b), scale, gin)
    return out, loss.reshape(()), gtok, gin, gbias.reshape(COLS), gout


def solution(mesh):
    torus = Mesh(mesh.devices.reshape(4, 4, 4, 2), AXES)
    placed = (P(AXES, None), P(AXES, None), P(AXES), P(AXES), P(), P(), P())
    return jax.shard_map(
        shards,
        mesh=torus,
        in_specs=placed,
        out_specs=(P(AXES, None), P(), P(AXES, None), P(), P(), P()),
        check_vma=False,
    )
```

time: 210 us -> 206 us (0.981)
  blocking collectives: 57.9 us -> 0 us
  starting transfers between devices: 1.5 us -> 38.4 us
  Pallas kernels: 56.7 us -> 73.2 us
  between operations: 14 us -> 0.91 us
  waiting for transfers between devices: 74.5 us -> 83 us
  local copies, waits for them, and re-layouts: 3.83 us -> 9.18 us
    all_to_all x0 -> x4, waiting for transfers between devices: none -> 79.3 us  [exchange(): return lax.all_to_all(value, CHIPS, 0, 0, tiled=True)]
    all_gather x1 -> x0, waiting for transfers between devices: 67.9 us -> none  [shards(): lax.all_gather(piece, AXES, axis=0, tiled=False)]
    all_to_all x1 -> x0, blocking collectives: 57.9 us -> none  [shards(): spread = lax.all_to_all(both, CHIPS, 0, 0, tiled=True)]
    all_to_all x0 -> x4, starting transfers between devices: none -> 30.1 us  [exchange(): return lax.all_to_all(value, CHIPS, 0, 0, tiled=True)]
    pallas_call x3 -> x8, Pallas kernels: 53 us -> 64.7 us  [the longest x1 20.9 us: forward_step(): pl.pallas_call(forward_kernel, in_specs=[SM, VM, VM, VM, HBM, VM, HBM], o...]
    unnamed x0 -> x24, local copies, waits for them, and re-layouts: none -> 9.18 us
    ppermute x1 -> x4, starting transfers between devices: 1.46 us -> 8.3 us  [swap(): return lax.ppermute(value, 'c', [(0, 1), (1, 0)])]
    pallas_call x1 -> x2, Pallas kernels: 3.65 us -> 8.51 us  [chip_sum(): pl.pallas_call(sum_kernel, grid=(PIECES // 16,), in_specs=[pl.BlockSpec((...]
  transfers between devices with their start and end apart: 2 -> 8, of which waited for: 2 -> 5; matrix products, arithmetic and copies ran while one was open for 0% -> 0% of each run, Pallas kernels for 0% -> 20%
where the time goes in v2:
time: 206 us; the launch traced here: 205 us
  waiting for transfers between devices  83 us (40%)
  Pallas kernels  73.2 us (36%)
  starting transfers between devices  38.4 us (19%)
  local copies, waits for them, and re-layouts  9.18 us (4%)
    all_to_all x4, waiting for transfers between devices, exchange(): return lax.all_to_all(value, CHIPS, 0, 0, tiled=True)  79.3 us
    all_to_all x4, starting transfers between devices, exchange(): return lax.all_to_all(value, CHIPS, 0, 0, tiled=True)  30.1 us
    pallas_call x1, Pallas kernels, forward_step(): pl.pallas_call(forward_kernel, in_specs=[SM, VM, VM, VM, HBM, VM, HBM], o...  20.9 us
    pallas_call x1, Pallas kernels, rows_step(): pl.pallas_call(rows_kernel, grid=(5,), in_specs=[pl.BlockSpec((ROWS, 512)...  10.1 us
    unnamed x24, local copies, waits for them, and re-layouts  9.18 us
    pallas_call x2, Pallas kernels, pair_add(): pl.pallas_call(pair_kernel, grid=(PIECES // 16,), in_specs=[spec, spec],...  8.66 us
    pallas_call x2, Pallas kernels, chip_sum(): pl.pallas_call(sum_kernel, grid=(PIECES // 16,), in_specs=[pl.BlockSpec((...  8.51 us
    ppermute x4, starting transfers between devices, swap(): return lax.ppermute(value, 'c', [(0, 1), (1, 0)])  8.3 us
  transfers between devices with their start and end apart: 8, of which 5 were waited for; matrix products, arithmetic and copies ran while one was open for 0% of the time, Pallas kernels for 20%

profile of v2, /device:TPU:1, one launch (start us, length us, event | category | flops | bytes accessed | tf_op | source)
XLA Modules:
  0.0 204.7 jit_solution(18428469062082327639)
XLA Ops:
  0.6 0.0 copy-start
  0.6 1.2 copy-done
  1.9 0.0 copy-start.1
  1.9 0.7 copy-done.1
  2.6 0.0 copy-start.2
  2.6 0.7 copy-done.2
  3.2 0.0 copy-start.3
  3.3 0.7 copy-done.3
  3.9 20.9 %forward_step.1 = (bf16[512,1024]{1,0:T(8,128)(2,1)}, bf16[64,136,128]{2,1,0:T(8,128)(2,1)}, bf16[64,136,128]{2,1,0:T(8,128)(2,1)}, bf16[1024,512]{1,0:T(8,128)(...) custom-call(s32[2]{0:T(128)S(1)} %copy-done.3, ...), custom_call_target="tpu_custom_call" | custom-call | flops 16000000000 | bytes 8388608 | tf_op jit(solution)/shard_map/forward_step/pallas_call | solution.py:214
  24.9 0.0 copy-start.4
  24.9 1.0 copy-done.4
  25.9 1.0 copy-done.5
  26.8 1.0 copy-done.6
  27.8 0.0 copy-start.7
  27.8 1.0 copy-done.7
  28.8 0.0 copy-start.8
  28.8 0.6 copy-done.8
  29.4 1.4 collective-permute-start
  30.8 6.2 %attention_back.1 = (bf16[512,1536]{1,0:T(8,128)(2,1)}, f32[1,1536]{1,0:T(1,128)}) custom-call(s32[2]{0:T(128)} %lens.3, bf16[512,1536]{1,0:T(8,128)(2,1)} %get-tuple-element.31.acts, bf16[512,1536]{1,0:T(8,128)(2,1)} %get-tuple-element.32.slope, bf16[512,1024]{1,0:T(8,128)(2,1)} %copy-done.7), custom_call_target="tpu_custom_call" | custom-call | flops 6000000000 | bytes 8388608 | tf_op jit(solution)/shard_map/attention_back/pallas_call | solution.py:273
  37.1 0.0 collective-permute-done.b
  37.1 0.0 copy-start.11
  37.1 1.4 copy-done.11
  38.4 4.5 %pair_add.2.after = bf16[64,136,128]{2,1,0:T(8,128)(2,1)} custom-call(bf16[64,136,128]{2,1,0:T(8,128)(2,1)} %get-tuple-element.28.a, bf16[64,136,128]{2,1,0:T(8,128)(2,1)} %copy-done.11), custom_call_target="tpu_custom_call" | custom-call | flops 2000000000 | bytes 8388608 | tf_op jit(solution)/shard_map/pair_add/pallas_call | solution.py:391
  42.9 11.4 %all-to-all-start = ((bf16[64,136,128]{2,1,0:T(8,128)(2,1)}), bf16[64,136,128]{2,1,0:T(8,128)(2,1)S(1)}, u32[]{:S(2)}, u32[]{:S(2)}) async-start(bf16[64,136,128]{2,1,0:T(8,128)(2,1)} %pair_add.2.after), calls=%async_computation | async-start | bytes 4456448 | tf_op jit(solution)/shard_map/all_to_all | solution.py:565
  54.4 5.3 %weights_step.1 = (bf16[64,104,128]{2,1,0:T(8,128)(2,1)}, bf16[64,104,128]{2,1,0:T(8,128)(2,1)}) custom-call(bf16[1024,512]{1,0:T(8,128)(2,1)} %copy-done.6, bf16[512,1536]{1,0:T(8,128)(2,1)} %get-tuple-element.34.dh.dhr, f32[1,1024]{1,0:T(1,128)} %copy-done.8, f32[1,1536]{1,0:T(1,128)} %get-tuple-element.38.bsum_r, bf16[64,136,128]{2,1,0:T(8,128)(2,1)} %pair_add.2.after), custom_call_target="tpu_custom_call" | custom-call | flops 4000000000 | bytes 8388608 | tf_op jit(solution)/shard_map/weights_step/pallas_call | solution.py:311
  59.6 0.4 collective-permute-start.2
  60.0 3.7 %collective-permute-done.2.b = bf16[64,104,128]{2,1,0:T(8,128)(2,1)} collective-permute-done((bf16[64,104,128]{2,1,0:T(8,128)(2,1)}, bf16[64,104,128]{2,1,0:T(8,128)(2,1)}, u32[]{:S(2)}, u32[]{:S(2)}) %collective-permute-start.2) | collective-permute-done | bytes 1703968 | tf_op jit(solution)/shard_map/ppermute | solution.py:561
  63.7 4.2 %pair_add.3 = bf16[64,104,128]{2,1,0:T(8,128)(2,1)} custom-call(bf16[64,104,128]{2,1,0:T(8,128)(2,1)} %get-tuple-element.39.after.a, bf16[64,104,128]{2,1,0:T(8,128)(2,1)} %collective-permute-done.2.b), custom_call_target="tpu_custom_call" | custom-call | flops 2000000000 | bytes 8388608 | tf_op jit(solution)/shard_map/pair_add/pallas_call | solution.py:391
  67.8 16.5 %all-to-all-done.a = bf16[64,136,128]{2,1,0:T(8,128)(2,1)S(1)} async-done(((bf16[64,136,128]{2,1,0:T(8,128)(2,1)}), bf16[64,136,128]{2,1,0:T(8,128)(2,1)S(1)}, u32[]{:S(2)}, u32[]{:S(2)}) %all-to-all-start) | async-done | bytes 2228256 | tf_op jit(solution)/shard_map/all_to_all | solution.py:565
  84.3 0.0 copy-start.10
  84.3 6.6 %all-to-all-start.2 = ((bf16[64,104,128]{2,1,0:T(8,128)(2,1)}), bf16[64,104,128]{2,1,0:T(8,128)(2,1)}, u32[]{:S(2)}, u32[]{:S(2)}) async-start(bf16[64,104,128]{2,1,0:T(8,128)(2,1)} %pair_add.3), calls=%async_computation.2 | async-start | bytes 3407872 | tf_op jit(solution)/shard_map/all_to_all | solution.py:565
  90.8 0.0 copy-done.10
  90.9 4.5 %chip_sum.2 = bf16[64,136,128]{2,1,0:T(8,128)(2,1)} custom-call(bf16[64,136,128]{2,1,0:T(8,128)(2,1)} %copy-done.10), custom_call_target="tpu_custom_call" | custom-call | flops 2000000000 | bytes 8388608 | tf_op jit(solution)/shard_map/chip_sum/pallas_call | solution.py:425
  95.3 18.9 %all-to-all-done.2.a = bf16[64,104,128]{2,1,0:T(8,128)(2,1)} async-done(((bf16[64,104,128]{2,1,0:T(8,128)(2,1)}), bf16[64,104,128]{2,1,0:T(8,128)(2,1)}, u32[]{:S(2)}, u32[]{:S(2)}) %all-to-all-start.2) | async-done | bytes 1703968 | tf_op jit(solution)/shard_map/all_to_all | solution.py:565
  114.2 5.3 %all-to-all-start.1 = ((bf16[64,136,128]{2,1,0:T(8,128)(2,1)}), bf16[64,136,128]{2,1,0:T(8,128)(2,1)S(1)}, u32[]{:S(2)}, u32[]{:S(2)}) async-start(bf16[64,136,128]{2,1,0:T(8,128)(2,1)} %chip_sum.2), calls=%async_computation.1 | async-start | bytes 4456448 | tf_op jit(solution)/shard_map/all_to_all | solution.py:565
  119.5 4.0 %chip_sum.3 = bf16[64,104,128]{2,1,0:T(8,128)(2,1)} custom-call(bf16[64,104,128]{2,1,0:T(8,128)(2,1)} %all-to-all-done.2.a), custom_call_target="tpu_custom_call" | custom-call | flops 2000000000 | bytes 8388608 | tf_op jit(solution)/shard_map/chip_sum/pallas_call | solution.py:425
  123.6 24.2 %all-to-all-done.1.own.tail = bf16[64,136,128]{2,1,0:T(8,128)(2,1)S(1)} async-done(((bf16[64,136,128]{2,1,0:T(8,128)(2,1)}), bf16[64,136,128]{2,1,0:T(8,128)(2,1)S(1)}, u32[]{:S(2)}, u32[]{:S(2)}) %all-to-all-start.1) | async-done | bytes 2228256 | tf_op jit(solution)/shard_map/all_to_all | solution.py:565
  147.8 0.0 copy-start.9
  147.8 6.8 %all-to-all-start.3 = ((bf16[64,104,128]{2,1,0:T(8,128)(2,1)}), bf16[64,104,128]{2,1,0:T(8,128)(2,1)}, u32[]{:S(2)}, u32[]{:S(2)}) async-start(bf16[64,104,128]{2,1,0:T(8,128)(2,1)} %chip_sum.3), calls=%async_computation.3 | async-start | bytes 3407872 | tf_op jit(solution)/shard_map/all_to_all | solution.py:565
  154.6 2.9 %collective-permute-start.1 = (bf16[64,136,128]{2,1,0:T(8,128)(2,1)S(1)}, bf16[64,136,128]{2,1,0:T(8,128)(2,1)}, u32[]{:S(2)}, u32[]{:S(2)}) collective-permute-start(bf16[64,136,128]{2,1,0:T(8,128)(2,1)S(1)} %all-to-all-done.1.own.tail), channel_id=1, source_target_pairs={{0,1},{1,0},{2,3},{3,2},{4,5},{5,4},{6,7},{7,6},{8,9},{9,8},{10,11... | collective-permute-start | bytes 6684680 | tf_op jit(solution)/shard_map/ppermute | solution.py:561
  157.6 19.8 %all-to-all-done.3.own.tail = bf16[64,104,128]{2,1,0:T(8,128)(2,1)} async-done(((bf16[64,104,128]{2,1,0:T(8,128)(2,1)}), bf16[64,104,128]{2,1,0:T(8,128)(2,1)}, u32[]{:S(2)}, u32[]{:S(2)}) %all-to-all-start.3) | async-done | bytes 1703968 | tf_op jit(solution)/shard_map/all_to_all | solution.py:565
  177.3 3.6 %collective-permute-start.3 = (bf16[64,104,128]{2,1,0:T(8,128)(2,1)}, bf16[64,104,128]{2,1,0:T(8,128)(2,1)}, u32[]{:S(2)}, u32[]{:S(2)}) collective-permute-start(bf16[64,104,128]{2,1,0:T(8,128)(2,1)} %all-to-all-done.3.own.tail), channel_id=1, source_target_pairs={{0,1},{1,0},{2,3},{3,2},{4,5},{5,4},{6,7},{7,6},{8,9},{9,8},{10,11... | collective-permute-start | bytes 5111816 | tf_op jit(solution)/shard_map/ppermute | solution.py:561
  181.0 10.1 %rows_step.1.dx = f32[512,1024]{1,0:T(8,128)} custom-call(bf16[512,1024]{1,0:T(8,128)(2,1)} %copy-done.5, bf16[512,1536]{1,0:T(8,128)(2,1)} %get-tuple-element.34.dh.dhr, bf16[1024,2560]{1,0:T(8,128)(2,1)} %win.1, bf16[512,1024]{1,0:T(8,128)(2,1)} %tok.3, bf16[512,1024]{1,0:T(8,128)(2,1)} %copy-done.4, bf16[64,104,128]{2,1,0:T(8,128)(2,1)} %get-tuple-element.39.after.a), custom_call_target="tpu_custom_call" | custom-call | flops 6000000000 | bytes 8388608 | tf_op jit(solution)/shard_map/rows_step/pallas_call | solution.py:358
  191.1 0.0 copy-done.9
  191.1 0.0 collective-permute-done.1.other
  191.1 6.6 %finish_a.1 = (bf16[1024,2560]{1,0:T(8,128)(2,1)}, bf16[1024,1024]{1,0:T(8,128)(2,1)}, bf16[512,1024]{1,0:T(8,128)(2,1)}, f32[8,128]{1,0:T(8,128)}, f32[1,1]{1,0:T(1,128)}) custom-call(bf16[64,136,128]{2,1,0:T(8,128)(2,1)} %copy-done.9, bf16[64,136,128]{2,1,0:T(8,128)(2,1)} %collective-permute-done.1.other, bf16[64,136,128]{2,1,0:T(8,128)(2,1)} %copy-done.9, ...), custom_call_target="tpu_custom_call" | custom-call | flops 3000000000 | bytes 8388608 | tf_op jit(solution)/shard_map/finish_a/pallas_call | solution.py:474
  197.7 0.0 collective-permute-done.3.other
  197.7 6.9 %finish_b.1 = (bf16[1024,2560]{1,0:T(8,128)(2,1)}, f32[20,128]{1,0:T(8,128)}) custom-call(bf16[64,104,128]{2,1,0:T(8,128)(2,1)} %all-to-all-done.3.own.tail, bf16[64,104,128]{2,1,0:T(8,128)(2,1)} %collective-permute-done.3.other, bf16[64,104,128]{2,1,0:T(8,128)(2,1)} %all-to-all-done.3.own.tail, ...), custom_call_target="tpu_custom_call", output_to_operand_aliasing={{0}: (4, {})} | custom-call | flops 3000000000 | bytes 8388608 | tf_op jit(solution)/shard_map/finish_b/pallas_call | solution.py:541
  (2 shorter events, 0.0 us)
Async XLA Ops:
  0.6 1.2 copy-start
  1.9 0.7 copy-start.1
  2.6 0.7 copy-start.2
  3.2 0.7 copy-start.3
  24.9 1.0 copy-start.4
  25.9 1.0 copy-start.5
  26.8 1.0 copy-start.6
  27.8 1.0 copy-start.7
  28.8 0.6 copy-start.8
  29.4 7.6 %collective-permute-start = (bf16[64,136,128]{2,1,0:T(8,128)(2,1)}, bf16[64,136,128]{2,1,0:T(8,128)(2,1)S(1)}, u32[]{:S(2)}, u32[]{:S(2)}) collective-permute-start(bf16[64,136,128]{2,1,0:T(8,128)(2,1)} %get-tuple-element.29), channel_id=1, source_target_pairs={{0,1},{1,0},{2,3},{3,2},{4,5},{5,4},{6,7},{7,6},{8,9},{9,8},{10,11... | collective-permute-start | bytes 6684680 | tf_op jit(solution)/shard_map/ppermute | solution.py:561
  37.1 1.4 copy-start.11
  42.9 41.3 %all-to-all-start = ((bf16[64,136,128]{2,1,0:T(8,128)(2,1)}), bf16[64,136,128]{2,1,0:T(8,128)(2,1)S(1)}, u32[]{:S(2)}, u32[]{:S(2)}) async-start(bf16[64,136,128]{2,1,0:T(8,128)(2,1)} %pair_add.2.after), calls=%async_computation | async-start | bytes 4456448 | tf_op jit(solution)/shard_map/all_to_all | solution.py:565
  59.6 4.0 %collective-permute-start.2 = (bf16[64,104,128]{2,1,0:T(8,128)(2,1)}, bf16[64,104,128]{2,1,0:T(8,128)(2,1)}, u32[]{:S(2)}, u32[]{:S(2)}) collective-permute-start(bf16[64,104,128]{2,1,0:T(8,128)(2,1)} %get-tuple-element.42), channel_id=1, source_target_pairs={{0,1},{1,0},{2,3},{3,2},{4,5},{5,4},{6,7},{7,6},{8,9},{9,8},{10,11... | collective-permute-start | bytes 5111816 | tf_op jit(solution)/shard_map/ppermute | solution.py:561
  84.3 6.6 %copy-start.10 = (bf16[64,136,128]{2,1,0:T(8,128)(2,1)}, bf16[64,136,128]{2,1,0:T(8,128)(2,1)S(1)}, u32[]{:S(2)}) copy-start(bf16[64,136,128]{2,1,0:T(8,128)(2,1)S(1)} %all-to-all-done.a) | copy-start | bytes 6684676
  84.3 30.0 %all-to-all-start.2 = ((bf16[64,104,128]{2,1,0:T(8,128)(2,1)}), bf16[64,104,128]{2,1,0:T(8,128)(2,1)}, u32[]{:S(2)}, u32[]{:S(2)}) async-start(bf16[64,104,128]{2,1,0:T(8,128)(2,1)} %pair_add.3), calls=%async_computation.2 | async-start | bytes 3407872 | tf_op jit(solution)/shard_map/all_to_all | solution.py:565
  114.2 33.5 %all-to-all-start.1 = ((bf16[64,136,128]{2,1,0:T(8,128)(2,1)}), bf16[64,136,128]{2,1,0:T(8,128)(2,1)S(1)}, u32[]{:S(2)}, u32[]{:S(2)}) async-start(bf16[64,136,128]{2,1,0:T(8,128)(2,1)} %chip_sum.2), calls=%async_computation.1 | async-start | bytes 4456448 | tf_op jit(solution)/shard_map/all_to_all | solution.py:565
  147.8 43.3 %copy-start.9 = (bf16[64,136,128]{2,1,0:T(8,128)(2,1)}, bf16[64,136,128]{2,1,0:T(8,128)(2,1)S(1)}, u32[]{:S(2)}) copy-start(bf16[64,136,128]{2,1,0:T(8,128)(2,1)S(1)} %all-to-all-done.1.own.tail) | copy-start | bytes 6684676
  147.8 29.6 %all-to-all-start.3 = ((bf16[64,104,128]{2,1,0:T(8,128)(2,1)}), bf16[64,104,128]{2,1,0:T(8,128)(2,1)}, u32[]{:S(2)}, u32[]{:S(2)}) async-start(bf16[64,104,128]{2,1,0:T(8,128)(2,1)} %chip_sum.3), calls=%async_computation.3 | async-start | bytes 3407872 | tf_op jit(solution)/shard_map/all_to_all | solution.py:565
  154.6 36.5 %collective-permute-start.1 = (bf16[64,136,128]{2,1,0:T(8,128)(2,1)S(1)}, bf16[64,136,128]{2,1,0:T(8,128)(2,1)}, u32[]{:S(2)}, u32[]{:S(2)}) collective-permute-start(bf16[64,136,128]{2,1,0:T(8,128)(2,1)S(1)} %all-to-all-done.1.own.tail), channel_id=1, source_target_pairs={{0,1},{1,0},{2,3},{3,2},{4,5},{5,4},{6,7},{7,6},{8,9},{9,8},{10,11... | collective-permute-start | bytes 6684680 | tf_op jit(solution)/shard_map/ppermute | solution.py:561
  177.3 20.3 %collective-permute-start.3 = (bf16[64,104,128]{2,1,0:T(8,128)(2,1)}, bf16[64,104,128]{2,1,0:T(8,128)(2,1)}, u32[]{:S(2)}, u32[]{:S(2)}) collective-permute-start(bf16[64,104,128]{2,1,0:T(8,128)(2,1)} %all-to-all-done.3.own.tail), channel_id=1, source_target_pairs={{0,1},{1,0},{2,3},{3,2},{4,5},{5,4},{6,7},{7,6},{8,9},{9,8},{10,11... | collective-permute-start | bytes 5111816 | tf_op jit(solution)/shard_map/ppermute | solution.py:561
